TPU v7x, 128 devices: a whole 4x4x4 slice. The times are simulated.
128 devices in a mesh: psr: 16 (over x, z), toa: 8 (over y, core).
Axes of the slice: x: 4, y: 4, z: 4, core: 2. Of those that a mesh axis runs over, the one named last changes fastest.
Arguments:
- design: bfloat16 [12288, 128, 256], P(('psr', 'toa')), may hold values from -0.035888672 to 0.035888672
- noise_weight: float32 [12288, 128], P(('psr', 'toa')), may hold values from 0.3 to 3
- residuals: bfloat16 [12288, 128], P(('psr', 'toa')), may hold values from -6 to 6
- slot_pulsar: int32 [12288], P(('psr', 'toa')), may hold values from 0 to 7, as said below
- slot_rows: int32 [12288], P(('psr', 'toa')), may hold values from 0 to 128, as said below
- own_prior: float32 [128, 192], P(('psr', 'toa')), may hold values from 0.2 to 5
- spectrum: float32 [32], replicated, may hold values from 0.05 to 2
- directions: float32 [3, 128], replicated, may hold values from -1 to 1, as said below
Outputs:
- coeffs: float32 [128, 64], P(('psr', 'toa'))
- log_dets: float32 [128], P(('psr', 'toa'))
- chi_square: float32 [128], P(('psr', 'toa'))
Inputs may be any that keep to these rules, and one draw needn't show every extreme that they name: `slot_pulsar`: pulsar k of group g is pulsar g * 8 + k of the arrays with a pulsar dimension; empty blocks name pulsar 0. `slot_rows`: on each device the blocks holding TOAs come first and the empty ones (0 rows) last; within a psr group a pulsar's blocks are consecutive in device order, cyclically, all full but its last; every pulsar has between 8 * 96 * 4 and 8 * 96 * 16 TOAs. `directions`: unit vectors; any two are at least 0.1 radians apart.
All inputs are finite; a program needn't handle non-finite values.
Results may differ from a plain program's by a relative error of at most 0.003.
Values sent between devices are 32-bit elements; how exact they have to be, the bound alone decides.
No kernel may reach another device: no remote copies, remote signals or barrier semaphores. Data moves between devices by JAX's collectives and lax.ppermute only.
A program may use at most 128 MiB of HBM per device.

v0:
```python
import math

import jax
import jax.numpy as jnp
from jax import lax
from jax.sharding import PartitionSpec as P

GROUP_PULSARS = 8
ITERS = 8


highest = lax.Precision.HIGHEST


def in_one_piece(arrays, axis, dim, along):
    ends, at = ([], 0)
    for a in arrays[:-1]:
        at += a.shape[along]
        ends.append(at)
    both = jnp.concatenate(arrays, axis=along)
    return tuple(jnp.split(lax.all_gather(both, axis, axis=dim, tiled=True), ends, axis=along))


def cut_along(value, dim, length):
    before, after = (value.shape[:dim], value.shape[dim + 1 :])
    return jnp.moveaxis(value.reshape(*before, length, -1, *after), dim, 0)


def sent_and_summed(value, axis, dim):
    length = lax.axis_size(axis)
    blocks = lax.all_to_all(cut_along(value, dim, length), axis, 0, 0, tiled=True)
    return jnp.sum(blocks, axis=0)


def in_one_piece_2(arrays, axis, dim, along):
    widths = [math.prod(a.shape[along:]) for a in arrays]
    both = jnp.concatenate(
        [a.reshape(*a.shape[:along], w) for a, w in zip(arrays, widths)], axis=along
    )
    filled = sent_and_summed(both, axis, dim)
    blocks = jnp.split(filled, [sum(widths[:k]) for k in range(1, len(widths))], axis=along)
    return tuple(
        (b.reshape(*filled.shape[:along], *a.shape[along:]) for a, b in zip(arrays, blocks))
    )


def cholesky_solve(factor, right_side):
    halfway = lax.linalg.triangular_solve(factor, right_side, left_side=True, lower=True)
    return lax.linalg.triangular_solve(
        factor, halfway, left_side=True, lower=True, transpose_a=True
    )


def slot_term_values(design, weight, residuals, pulsar, slot_rows):
    positions = lax.broadcasted_iota(jnp.int32, weight.shape, 1)
    weight = jnp.where(positions < slot_rows[:, None], weight, 0.0)
    weighted = (weight[:, :, None] * design).astype(jnp.bfloat16)
    products = jnp.einsum("srk,srl->skl", weighted, design, preferred_element_type=jnp.float32)
    fitted = jnp.einsum("srk,sr->sk", weighted, residuals, preferred_element_type=jnp.float32)
    widened = residuals.astype(jnp.float32)
    energy = jnp.sum(weight * widened * widened, axis=1)
    owners = (
        pulsar[:, None] == lax.broadcasted_iota(jnp.int32, (pulsar.shape[0], GROUP_PULSARS), 1)
    ).astype(jnp.float32)
    return (
        jnp.einsum("sp,skl->pkl", owners, products, precision=highest),
        jnp.einsum("sp,sk->pk", owners, fitted, precision=highest),
        jnp.dot(energy, owners, precision=highest),
        jnp.dot(slot_rows.astype(jnp.float32), owners, precision=highest),
    )


def local_grams(design, noise_weight, residuals, slot_pulsar, slot_rows):
    column_count = design.shape[2]
    used_slots = jnp.sum((slot_rows > 0).astype(jnp.int32))
    block_count = (used_slots + 15) // 16
    initial = (
        jnp.zeros((GROUP_PULSARS, column_count, column_count), jnp.float32),
        jnp.zeros((GROUP_PULSARS, column_count), jnp.float32),
        jnp.zeros((GROUP_PULSARS,), jnp.float32),
        jnp.zeros((GROUP_PULSARS,), jnp.float32),
    )

    def one_block(block_index, running_total):
        offset = block_index * 16
        term_pieces = [
            lax.dynamic_slice_in_dim(member, offset, 16, 0)
            for member in (design, noise_weight, residuals, slot_pulsar, slot_rows)
        ]
        summand_terms = slot_term_values(*term_pieces)
        return tuple(
            (
                earlier_term + later_term
                for earlier_term, later_term in zip(running_total, summand_terms)
            )
        )

    return lax.fori_loop(0, block_count, one_block, initial)


def eliminate(gram_sums, projections, own_prior):
    column_count = gram_sums.shape[1]
    common = column_count - own_prior.shape[1]
    identity = jnp.eye(own_prior.shape[1], dtype=jnp.float32)
    own_block = (
        gram_sums[:, common:, common:] + (1.0 / own_prior)[:, :, None] * identity[None, :, :]
    )
    factor = jnp.linalg.cholesky(own_block)
    right_side = jnp.concatenate(
        [gram_sums[:, common:, :common], projections[:, common:, None]], axis=2
    )
    solved = cholesky_solve(factor, right_side)
    cross_block = gram_sums[:, :common, common:]
    reduced = jnp.einsum("pck,pkd->pcd", cross_block, solved, precision=highest)
    schur_part = gram_sums[:, :common, :common] - reduced[:, :, :common]
    target = projections[:, :common] - reduced[:, :, common]
    quadratic = jnp.sum(projections[:, common:] * solved[:, :, common], axis=1)
    own_logdet = 2.0 * jnp.sum(jnp.log(jnp.diagonal(factor, axis1=1, axis2=2)), axis=1)
    return (schur_part, target, quadratic, own_logdet)


def coupling_inverse(directions):
    cosines = jnp.clip(jnp.dot(directions.T, directions, precision=highest), -1.0, 1.0)
    number = cosines.shape[0]
    diagonal = jnp.eye(number, dtype=jnp.float32) > 0.5
    spread = jnp.where(diagonal, 1.0, 0.5 * (1.0 - cosines))
    intersect_curve = 1.5 * spread * jnp.log(spread) - 0.25 * spread + 0.5
    correlation = jnp.where(diagonal, 1.0, intersect_curve)
    factor = jnp.linalg.cholesky(correlation)
    return cholesky_solve(factor, jnp.eye(number, dtype=jnp.float32))


def precondition(block_factor, residual):
    return cholesky_solve(block_factor, residual[:, :, None])[:, :, 0]


def block_setup(schur_part, self_coupling, inverse_power):
    block_matrix = schur_part + self_coupling[:, None, None] * jnp.diag(inverse_power)[None, :, :]
    block_factor = jnp.linalg.cholesky(block_matrix)
    block_logdet = 2.0 * jnp.sum(jnp.log(jnp.diagonal(block_factor, axis1=1, axis2=2)), axis=1)
    return (block_factor, block_logdet)


def share_scaled(scaled, stats):
    return in_one_piece((scaled, stats), ("psr", "toa"), 0, 1)


def conjugate_shared(
    schur_part, target, coupling, self_coupling, inverse_power, first_pulsar, owned_count
):
    block_factor, block_logdet = block_setup(schur_part, self_coupling, inverse_power)
    solution = jnp.zeros_like(target)
    residual = target
    scaled = precondition(block_factor, residual)
    within_scaled = jnp.einsum("pcd,pd->pc", schur_part, scaled, precision=highest)
    stats = jnp.stack(
        [
            jnp.sum(residual * scaled, axis=1),
            jnp.sum(scaled * within_scaled, axis=1),
            jnp.zeros((owned_count,), jnp.float32),
        ],
        axis=1,
    )
    direction, gathered_stats = share_scaled(scaled, stats)
    inner_now = jnp.sum(gathered_stats[:, 0])
    curved = gathered_stats[:, 1]
    for iteration in range(ITERS):
        mixing = jnp.dot(coupling, direction, precision=highest)
        curvature = jnp.sum(curved) + jnp.sum(direction * mixing * inverse_power[None, :])
        own_direction = lax.dynamic_slice_in_dim(direction, first_pulsar, owned_count, 0)
        own_mixing = lax.dynamic_slice_in_dim(mixing, first_pulsar, owned_count, 0)
        within_direction = jnp.einsum("pcd,pd->pc", schur_part, own_direction, precision=highest)
        mapped = within_direction + own_mixing * inverse_power[None, :]
        step_size = inner_now / curvature
        solution = solution + step_size * own_direction
        residual = residual - step_size * mapped
        if iteration + 1 < ITERS:
            scaled = precondition(block_factor, residual)
            within_scaled = jnp.einsum("pcd,pd->pc", schur_part, scaled, precision=highest)
            crossing = jnp.sum(scaled * within_direction, axis=1) + jnp.sum(
                own_direction * within_scaled, axis=1
            )
            stats = jnp.stack(
                [
                    jnp.sum(residual * scaled, axis=1),
                    jnp.sum(scaled * within_scaled, axis=1),
                    crossing,
                ],
                axis=1,
            )
            gathered_scaled, gathered_stats = share_scaled(scaled, stats)
            inner_next = jnp.sum(gathered_stats[:, 0])
            ratio = inner_next / inner_now
            direction = gathered_scaled + ratio * direction
            curved = gathered_stats[:, 1] + ratio * gathered_stats[:, 2] + ratio * ratio * curved
            inner_now = inner_next
    return (solution, block_logdet)


def body(design, noise_weight, residuals, slot_pulsar, slot_rows, own_prior, spectrum, directions):
    toa_devices = lax.axis_size("toa")
    owned_count = GROUP_PULSARS // toa_devices
    device = lax.axis_index("psr") * toa_devices + lax.axis_index("toa")
    first_pulsar = device * owned_count
    gram_part, fit_part, energy_part, count_part = local_grams(
        design, noise_weight, residuals, slot_pulsar, slot_rows
    )
    reduced_ready = False
    gram_sums, projections, energy, counts = in_one_piece_2(
        (gram_part, fit_part, energy_part, count_part), "toa", 0, 1
    )
    schur_part, target, quadratic, own_logdet = eliminate(gram_sums, projections, own_prior)
    coupling = coupling_inverse(directions)
    inverse_power = 1.0 / jnp.repeat(spectrum, 2)
    self_coupling = lax.dynamic_slice_in_dim(jnp.diagonal(coupling), first_pulsar, owned_count, 0)
    solution, block_logdet = conjugate_shared(
        schur_part, target, coupling, self_coupling, inverse_power, first_pulsar, owned_count
    )
    column_count = design.shape[2]
    log_dets = (own_logdet + block_logdet) / column_count
    chi_square = (energy - quadratic - jnp.sum(target * solution, axis=1)) / counts
    return (solution, log_dets, chi_square)


def solution(mesh):
    return jax.shard_map(
        body,
        mesh=mesh,
        in_specs=(
            P(("psr", "toa"), None, None),
            P(("psr", "toa"), None),
            P(("psr", "toa"), None),
            P(("psr", "toa")),
            P(("psr", "toa")),
            P(("psr", "toa"), None),
            P(),
            P(),
        ),
        out_specs=(P(("psr", "toa"), None), P(("psr", "toa")), P(("psr", "toa"))),
        check_vma=False,
    )
```

profile of v0, /device:TPU:1, one launch (start us, length us, event | category | flops | bytes accessed | tf_op | source)
XLA Modules:
  0.0 514.3 jit_solution(1389055020210524862)
XLA Ops:
  2.9 1.5 constant_dynamic-update-slice_fusion.2
  7.7 4.3 reshape.578
  12.1 73.7 %all-to-all-start = ((f32[8,1,65794]{2,1,0:T(1,128)}), f32[8,1,65794]{2,1,0:T(1,128)S(1)}, u32[]{:S(2)}, u32[]{:S(2)}) async-start(f32[8,1,65794]{2,1,0:T(1,128)} %reshape.578), calls=%async_computation | async-start | bytes 4218880 | tf_op jit(solution)/shard_map/all_to_all | solution.py:31
  86.6 11.7 %cholesky.215 = f32[128,128]{1,0:T(8,128)S(1)} custom-call(f32[128,128]{1,0:T(8,128)S(1)} %add_multiply_fusion), custom_call_target="Cholesky" | custom-call | tf_op jit(solution)/shard_map/jit(cholesky)/cholesky | solution.py:129
  99.6 9.8 %custom-call.40 = f32[1,128,128]{1,2,0:T(8,128)S(1)} custom-call(f32[1,128,128]{2,1,0:T(8,128)S(1)} %fusion.40), custom_call_target="InvertDiagBlocksLowerTriangular" | custom-call | tf_op jit(solution)/shard_map/triangular_solve | solution.py:49
  109.9 1.5 gather_fusion
  112.1 1.5 reduce_sum.556
  115.7 11.7 %custom-call.36 = f32[1,128,128]{2,1,0:T(8,128)S(1)} custom-call(f32[1,128,128]{2,1,0:T(8,128)S(1)} %cholesky.231), custom_call_target="Cholesky" | custom-call | tf_op jit(solution)/shard_map/jit(cholesky)/cholesky | solution.py:108
  127.5 9.8 %custom-call.37 = f32[1,1,128,128]{2,3,1,0:T(8,128)S(1)} custom-call(f32[1,1,128,128]{3,2,1,0:T(8,128)S(1)} %get-tuple-element.165), custom_call_target="InvertDiagBlocksLowerTriangular" | custom-call | tf_op jit(solution)/shard_map/jit(cholesky)/cholesky | solution.py:108
  137.7 5.8 %custom-call.38 = f32[1,64,64]{2,1,0:T(8,128)S(1)} custom-call(f32[1,64,64]{2,1,0:T(8,128)S(1)} %fusion.29), custom_call_target="Cholesky" | custom-call | tf_op jit(solution)/shard_map/jit(cholesky)/cholesky | solution.py:108
  146.3 19.9 %custom-call.39 = f32[1,2,128,128]{2,3,1,0:T(8,128)S(1)} custom-call(f32[1,2,128,128]{3,2,1,0:T(8,128)S(1)} %pad_maximum_fusion), custom_call_target="InvertDiagBlocksLowerTriangular" | custom-call | tf_op jit(solution)/shard_map/triangular_solve | solution.py:49
  170.0 5.8 %custom-call.41 = f32[1,64,64]{2,1,0:T(8,128)S(1)} custom-call(f32[1,64,64]{2,1,0:T(8,128)S(1)} %fusion.120), custom_call_target="Cholesky" | custom-call | tf_op jit(solution)/shard_map/jit(cholesky)/cholesky | solution.py:139
  177.2 4.9 custom-call.63
  185.1 33.2 %all-gather = f32[128,1,67]{2,1,0:T(1,128)S(1)} all-gather(f32[1,1,67]{2,1,0:T(1,128)S(1)} %maximum_bitcast_fusion), channel_id=1, replica_groups=mesh['psr'=16,'toa'=8] {'psr','toa'}, dimensions={0}, use_global_device_ids=true | all-gather | bytes 34572 | tf_op jit(solution)/shard_map/all_gather | solution.py:21
  225.6 1.4 maximum_bitcast_fusion.1
  227.0 29.7 %all-gather.1 = f32[128,1,67]{2,1,0:T(1,128)S(1)} all-gather(f32[1,1,67]{2,1,0:T(1,128)S(1)} %maximum_bitcast_fusion.1), channel_id=1, replica_groups=mesh['psr'=16,'toa'=8] {'psr','toa'}, dimensions={0}, use_global_device_ids=true | all-gather | bytes 34572 | tf_op jit(solution)/shard_map/all_gather | solution.py:21
  267.4 29.6 %all-gather.2 = f32[128,1,67]{2,1,0:T(1,128)S(1)} all-gather(f32[1,1,67]{2,1,0:T(1,128)S(1)} %maximum_bitcast_fusion.2), channel_id=1, replica_groups=mesh['psr'=16,'toa'=8] {'psr','toa'}, dimensions={0}, use_global_device_ids=true | all-gather | bytes 34572 | tf_op jit(solution)/shard_map/all_gather | solution.py:21
  306.3 1.4 maximum_bitcast_fusion.3
  307.7 29.3 %all-gather.3 = f32[128,1,67]{2,1,0:T(1,128)S(1)} all-gather(f32[1,1,67]{2,1,0:T(1,128)S(1)} %maximum_bitcast_fusion.3), channel_id=1, replica_groups=mesh['psr'=16,'toa'=8] {'psr','toa'}, dimensions={0}, use_global_device_ids=true | all-gather | bytes 34572 | tf_op jit(solution)/shard_map/all_gather | solution.py:21
  347.7 29.3 %all-gather.4 = f32[128,1,67]{2,1,0:T(1,128)S(1)} all-gather(f32[1,1,67]{2,1,0:T(1,128)S(1)} %maximum_bitcast_fusion.4), channel_id=1, replica_groups=mesh['psr'=16,'toa'=8] {'psr','toa'}, dimensions={0}, use_global_device_ids=true | all-gather | bytes 34572 | tf_op jit(solution)/shard_map/all_gather | solution.py:21
  387.8 29.3 %all-gather.5 = f32[128,1,67]{2,1,0:T(1,128)S(1)} all-gather(f32[1,1,67]{2,1,0:T(1,128)S(1)} %maximum_bitcast_fusion.5), channel_id=1, replica_groups=mesh['psr'=16,'toa'=8] {'psr','toa'}, dimensions={0}, use_global_device_ids=true | all-gather | bytes 34572 | tf_op jit(solution)/shard_map/all_gather | solution.py:21
  427.8 29.3 %all-gather.6 = f32[128,1,67]{2,1,0:T(1,128)S(1)} all-gather(f32[1,1,67]{2,1,0:T(1,128)S(1)} %maximum_bitcast_fusion.6), channel_id=1, replica_groups=mesh['psr'=16,'toa'=8] {'psr','toa'}, dimensions={0}, use_global_device_ids=true | all-gather | bytes 34572 | tf_op jit(solution)/shard_map/all_gather | solution.py:21
  467.8 29.4 %all-gather.7 = f32[128,1,67]{2,1,0:T(1,128)S(1)} all-gather(f32[1,1,67]{2,1,0:T(1,128)S(1)} %maximum_bitcast_fusion.7), channel_id=1, replica_groups=mesh['psr'=16,'toa'=8] {'psr','toa'}, dimensions={0}, use_global_device_ids=true | all-gather | bytes 34572 | tf_op jit(solution)/shard_map/all_gather | solution.py:21
  505.3 1.9 gather_fusion.1
  (159 shorter events, 65.1 us)
Async XLA Ops:
  0.6 85.5 %copy-start = (f32[3,128]{1,0:T(4,128)S(1)}, f32[3,128]{1,0:T(4,128)}, u32[]{:S(2)}) copy-start(f32[3,128]{1,0:T(4,128)} %param.21) | copy-start | bytes 4612
  0.6 2.2 copy-start.2
  0.7 2.2 copy-start.3
  12.1 73.7 %copy-start.4 = (f32[32]{0:T(128)S(1)}, f32[32]{0:T(128)}, u32[]{:S(2)}) copy-start(f32[32]{0:T(128)} %param.20) | copy-start | bytes 388
  12.1 99.9 %copy-start.1 = (f32[1,192]{1,0:T(1,128)S(1)}, f32[1,192]{1,0:T(1,128)}, u32[]{:S(2)}) copy-start(f32[1,192]{1,0:T(1,128)} %param.19) | copy-start | bytes 2308
  12.1 100.0 %all-to-all-start = ((f32[8,1,65794]{2,1,0:T(1,128)}), f32[8,1,65794]{2,1,0:T(1,128)S(1)}, u32[]{:S(2)}, u32[]{:S(2)}) async-start(f32[8,1,65794]{2,1,0:T(1,128)} %reshape.578), calls=%async_computation | async-start | bytes 4218880 | tf_op jit(solution)/shard_map/all_to_all | solution.py:31
where the time goes:
time: 523 us; the launch traced here: 514 us
  blocking collectives  239 us (46%)
  other arithmetic  117 us (22%)
  starting transfers between devices  73.7 us (14%)
  between operations  43.4 us (8%)
  matrix products  24 us (5%)
  local copies, waits for them, and re-layouts  16.8 us (3%)
    all_gather x8, blocking collectives, in_one_piece(): lax.all_gather(both, axis, axis=dim, tiled=True)  239 us
    all_to_all x1, starting transfers between devices, sent_and_summed(): lax.all_to_all(cut_along(value, dim, length), axis, 0, 0, tiled=True)  73.7 us
    another operation x8, other arithmetic, cholesky_solve(): lax.linalg.triangular_solve(factor, halfway, left_side=True, lower=True,...  35.4 us
    another operation x7, other arithmetic, eliminate(): factor = jnp.linalg.cholesky(own_block)  28.7 us
    another operation x3, other arithmetic, coupling_inverse(): factor = jnp.linalg.cholesky(correlation)  12.4 us
    unnamed x8, other arithmetic  11 us
  transfers between devices with their start and end apart: 1, of which 0 were waited for; matrix products, arithmetic and copies ran while one was open for 5% of the time, Pallas kernels for 0%

commit v1 on v0

v1 whole, which is shorter than its diff:
```python
import jax
import jax.numpy as jnp
from jax import lax
from jax.experimental import pallas as pl
from jax.experimental.pallas import tpu as pltpu
from jax.sharding import PartitionSpec as P

GROUP_PULSARS = 8
ITERS = 8
COLUMNS = 256
COMMON = 64
STEP_BLOCKS = 16
ROWS_SENT = 264
WIDTH = 2176
AXES = ("psr", "toa")

highest = lax.Precision.HIGHEST
f32 = jnp.float32


def iota(shape, dim):
    return lax.broadcasted_iota(jnp.int32, shape, dim)


def sub_bcast(value, row):
    return jnp.broadcast_to(value[row : row + 1, :], value.shape)


def lane_bcast(value, lane):
    return jnp.broadcast_to(value[:, lane : lane + 1], value.shape)


def total(value):
    return jnp.sum(jnp.sum(value, axis=0, keepdims=True), axis=1, keepdims=True)


def eliminate_rows(tiles, first_lane, log_sum):
    count = len(tiles)
    width = len(tiles[0])
    row = iota((8, 128), 0)
    for b in range(count):
        at = first_lane + 8 * b
        tile, lane = at // 128, at % 128
        cols = [lane_bcast(tiles[b][tile], lane + k) for k in range(8)]
        for i in range(8):
            here = row == i
            pivot = sub_bcast(cols[i], i)
            inverse = 1.0 / pivot
            log_sum = log_sum + jnp.log(pivot)
            column = cols[i]
            for k in range(8):
                if k != i:
                    scaled = sub_bcast(cols[k], i) * inverse
                    cols[k] = jnp.where(here, scaled, cols[k] - column * scaled)
            cols[i] = jnp.where(here, inverse, -column * inverse)
        fresh = []
        for t in range(width):
            parts = [cols[k] * sub_bcast(tiles[b][t], k) for k in range(8)]
            while len(parts) > 1:
                parts = [u + v for u, v in zip(parts[::2], parts[1::2])]
            fresh.append(parts[0])
        spread = [[sub_bcast(fresh[t], k) for k in range(8)] for t in range(width)]
        for a in range(count):
            if a != b:
                factor = [lane_bcast(tiles[a][tile], lane + k) for k in range(8)]
                for t in range(width):
                    value = tiles[a][t]
                    for k in range(8):
                        value = value - factor[k] * spread[t][k]
                    tiles[a][t] = value
        tiles[b] = fresh
    return tiles, log_sum


def gram_kernel(
    pulsar_ref,
    rows_ref,
    place_ref,
    design_ref,
    weight_ref,
    resid_ref,
    mine_ref,
    other_ref,
    gram,
    fit,
    energy,
    wide_resid,
    counts,
):
    step = pl.program_id(0)

    @pl.when(step == 0)
    def _():
        gram[...] = jnp.zeros(gram.shape, f32)
        fit[...] = jnp.zeros(fit.shape, f32)
        energy[...] = jnp.zeros(energy.shape, f32)
        for k in range(GROUP_PULSARS):
            counts[k] = 0

    wide_resid[...] = resid_ref[...].astype(f32)
    lane = iota((1, 128), 1)

    def add_blocks(local, number, pulsar):
        pieces, fitted, squares = [], None, None
        for i in range(number):
            valid = rows_ref[step * STEP_BLOCKS + local + i]
            weight = jnp.where(lane < valid, weight_ref[pl.ds(local + i, 1), :], 0.0)
            resid = wide_resid[pl.ds(local + i, 1), :]
            turned = design_ref[local + i].T.astype(f32)
            weighted = (turned * weight).astype(jnp.bfloat16)
            pieces.append(weighted)
            product = weighted.astype(f32) * resid
            square = weight * resid * resid
            fitted = product if fitted is None else fitted + product
            squares = square if squares is None else squares + square
            counts[pulsar] = counts[pulsar] + valid
        left = jnp.concatenate(pieces, axis=1) if number > 1 else pieces[0]
        right = design_ref[pl.ds(local, number)].reshape(number * 128, COLUMNS)
        gram[pulsar] = gram[pulsar] + jnp.dot(left, right, preferred_element_type=f32)
        fit[pulsar] = fit[pulsar] + fitted
        energy[pl.ds(pulsar, 1), :] = energy[pl.ds(pulsar, 1), :] + squares

    def quad(q, carry):
        at = step * STEP_BLOCKS + q * 4
        pulsars = [pulsar_ref[at + i] for i in range(4)]
        filled = rows_ref[at] + rows_ref[at + 1] + rows_ref[at + 2] + rows_ref[at + 3] > 0
        same = (
            (pulsars[0] == pulsars[1])
            & (pulsars[1] == pulsars[2])
            & (pulsars[2] == pulsars[3])
        )

        @pl.when(filled & same)
        def _():
            add_blocks(q * 4, 4, pulsars[0])

        @pl.when(filled & jnp.logical_not(same))
        def _():
            for i in range(4):
                add_blocks(q * 4 + i, 1, pulsars[i])

        return carry

    lax.fori_loop(0, STEP_BLOCKS // 4, quad, 0)

    @pl.when(step == pl.num_programs(0) - 1)
    def _():
        row, col = iota((128, 128), 0), iota((128, 128), 1)
        line = iota((8, 128), 0)
        spot = iota((8, 128), 1)

        def pack(out_ref, s, k):
            @pl.when(counts[k] == 0)
            def _():
                out_ref[s] = jnp.zeros((ROWS_SENT, 128), f32)

            @pl.when(counts[k] > 0)
            def _():
                upper = gram[k, 0:128, 0:128]
                lower = gram[k, 128:256, 128:256]
                upper = 0.5 * (upper + upper.T)
                lower = 0.5 * (lower + lower.T)
                cross = 0.5 * (gram[k, 128:256, 0:128] + gram[k, 0:128, 128:256].T)
                out_ref[s, 0:128, :] = jnp.where(col > row, upper, lower)
                out_ref[s, 128:256, :] = cross
                diagonal = jnp.sum(jnp.where(col == row, upper, 0.0), axis=0, keepdims=True)
                first = jnp.sum(fit[k, 0:128, :].T, axis=0, keepdims=True)
                second = jnp.sum(fit[k, 128:256, :].T, axis=0, keepdims=True)
                power = jnp.sum(energy[pl.ds(k, 1), :], axis=1, keepdims=True)
                number = counts[k].astype(f32)
                last = jnp.where(spot == 0, power, jnp.where(spot == 1, number, 0.0))
                rest = jnp.where(line == 3, last, 0.0)
                rest = jnp.where(line == 0, diagonal, rest)
                rest = jnp.where(line == 1, first, rest)
                out_ref[s, 256:264, :] = jnp.where(line == 2, second, rest)

        height = place_ref[0]
        core = place_ref[1]
        for s in range(4):
            base = 2 * ((height + s) & 3)
            pack(mine_ref, s, base + core)
            pack(other_ref, s, base + 1 - core)


def gram_parts(place, design, weight, residuals, slot_pulsar, slot_rows):
    slots = design.shape[0]
    piece = jax.ShapeDtypeStruct((4, ROWS_SENT, 128), f32)
    whole = pl.BlockSpec((4, ROWS_SENT, 128), lambda i, *_: (0, 0, 0))
    return pl.pallas_call(
        gram_kernel,
        grid_spec=pltpu.PrefetchScalarGridSpec(
            num_scalar_prefetch=3,
            grid=(slots // STEP_BLOCKS,),
            in_specs=[
                pl.BlockSpec((STEP_BLOCKS, 128, COLUMNS), lambda i, *_: (i, 0, 0)),
                pl.BlockSpec((STEP_BLOCKS, 128), lambda i, *_: (i, 0)),
                pl.BlockSpec((STEP_BLOCKS, 128), lambda i, *_: (i, 0)),
            ],
            out_specs=[whole, whole],
            scratch_shapes=[
                pltpu.VMEM((GROUP_PULSARS, COLUMNS, COLUMNS), f32),
                pltpu.VMEM((GROUP_PULSARS, COLUMNS, 128), f32),
                pltpu.VMEM((GROUP_PULSARS, 128), f32),
                pltpu.VMEM((STEP_BLOCKS, 128), f32),
                pltpu.SMEM((GROUP_PULSARS,), jnp.int32),
            ],
        ),
        out_shape=[piece, piece],
        name="gram",
    )(slot_pulsar, slot_rows, place, design, weight, residuals)


def coupling_kernel(place_ref, directions_ref, out_ref):
    core = place_ref[1]
    row, col = iota((128, 128), 0), iota((128, 128), 1)
    source = jnp.where(col < 64, 2 * col + core, 2 * col - 127 - core)
    chosen = (row == source).astype(f32)
    lines = jnp.concatenate([directions_ref[...], jnp.zeros((5, 128), f32)], axis=0)
    lines = jnp.dot(lines, chosen, precision=highest, preferred_element_type=f32)
    turned = lines.T
    cosines = jnp.zeros((128, 128), f32)
    for i in range(3):
        cosines = cosines + turned[:, i : i + 1] * lines[i : i + 1, :]
    cosines = jnp.clip(cosines, -1.0, 1.0)
    same = row == col
    spread = jnp.where(same, 1.0, 0.5 * (1.0 - cosines))
    curve = 1.5 * spread * jnp.log(spread) - 0.25 * spread + 0.5
    correlation = jnp.where(same, 1.0, curve)
    identity = jnp.where(same, 1.0, 0.0)
    tiles = [
        [correlation[8 * a : 8 * a + 8, :], identity[8 * a : 8 * a + 8, :]] for a in range(16)
    ]
    tiles, _ = eliminate_rows(tiles, 0, jnp.zeros((8, 128), f32))
    for a in range(16):
        out_ref[8 * a : 8 * a + 8, :] = tiles[a][1]


def coupling_inverse(place, directions):
    return pl.pallas_call(
        coupling_kernel,
        in_specs=[
            pl.BlockSpec(memory_space=pltpu.SMEM),
            pl.BlockSpec(memory_space=pltpu.VMEM),
        ],
        out_specs=pl.BlockSpec(memory_space=pltpu.VMEM),
        out_shape=jax.ShapeDtypeStruct((128, 128), f32),
        name="coupling",
    )(place, directions)


def power_column(spectrum_ref):
    inverse = 1.0 / spectrum_ref[...]
    half = iota((64, 32), 0) >> 1
    spread = jnp.where(iota((64, 32), 1) == half, jnp.broadcast_to(inverse, (64, 32)), 0.0)
    return jnp.sum(spread, axis=1, keepdims=True)


def own_kernel(
    place_ref,
    part0,
    part1,
    part2,
    part3,
    prior_ref,
    spectrum_ref,
    coupling_ref,
    sent_ref,
    extra_ref,
    logdet_ref,
    work,
):
    row, col = iota((128, 128), 0), iota((128, 128), 1)

    def summed(lo, hi):
        return (part0[lo:hi, :] + part1[lo:hi, :]) + (part2[lo:hi, :] + part3[lo:hi, :])

    packed = summed(0, 128)
    cross = summed(128, 256)
    rest = summed(256, 264)
    turned = packed.T
    prior = 1.0 / prior_ref[...]
    prior = jnp.concatenate([jnp.zeros((1, 64), f32), prior], axis=1)
    upper = jnp.where(col > row, packed, turned)
    upper = jnp.where(col == row, rest[0:1, :] + prior[:, 0:128], upper)
    lower = jnp.where(col <= row, packed, turned)
    lower = jnp.where(col == row, lower + prior[:, 128:256], lower)
    work[0:128, 0:128] = upper
    work[128:256, 128:256] = lower
    work[128:256, 0:128] = cross
    work[0:128, 128:256] = cross.T
    side = rest.T
    work[0:128, 256:384] = jnp.broadcast_to(side[:, 1:2], (128, 128))
    work[128:256, 256:384] = jnp.broadcast_to(side[:, 2:3], (128, 128))

    log_sum = jnp.zeros((8, 128), f32)
    quadratic = jnp.zeros((64, 128), f32)
    for panel in range(3):
        at = COMMON + 64 * panel
        old = work[at : at + 64, :]
        tiles = [
            [old[8 * a : 8 * a + 8, 128 * t : 128 * t + 128] for t in range(3)] for a in range(8)
        ]
        tiles, log_sum = eliminate_rows(tiles, at, log_sum)
        fresh = [jnp.concatenate([tiles[a][t] for a in range(8)], axis=0) for t in range(3)]
        quadratic = quadratic + old[:, 256:384] * fresh[2]
        final = panel == 2
        for t in (0,) if final else (0, 1):
            left = old[:, 128 * t : 128 * t + 128]
            for u in (0, 2) if final else (0, 1, 2):
                change = lax.dot_general(
                    left,
                    fresh[u],
                    (((0,), (0,)), ((), ())),
                    precision=highest,
                    preferred_element_type=f32,
                )
                where = (slice(128 * t, 128 * t + 128), slice(128 * u, 128 * u + 128))
                work[where] = work[where] - change

    own = place_ref[2]
    mine = jnp.where((row == own) & (col == own), coupling_ref[...], 0.0)
    self_coupling = total(mine)
    power = power_column(spectrum_ref)
    row64, col64 = iota((64, 128), 0), iota((64, 128), 1)
    block = work[0:64, 0:128]
    block = jnp.where(row64 == col64, block + self_coupling * power, block)
    block = jnp.where(col64 < 64, block, jnp.where(col64 == row64 + 64, 1.0, 0.0))
    tiles = [[block[8 * a : 8 * a + 8, :]] for a in range(8)]
    tiles, log_sum = eliminate_rows(tiles, 0, log_sum)
    solved = jnp.concatenate([tiles[a][0] for a in range(8)], axis=0)
    inverse = pltpu.roll(solved, 64, 1)
    top, bottom = inverse[0:32, :], inverse[32:64, :]
    row32, col32 = iota((32, 128), 0), iota((32, 128), 1)
    moved = pltpu.roll(bottom, 96, 1)
    triangle = jnp.where(col32 > row32, top, moved)
    folded = jnp.where(col32 < 32, triangle, top)
    lines = jnp.where(
        iota((16, 128), 1) < 64, folded[0:16, :], pltpu.roll(folded[16:32, :], 64, 1)
    )
    diagonal = jnp.sum(jnp.where(row32 == col32, top, 0.0), axis=0, keepdims=True)
    target = work[0:64, 256:384]
    target_line = jnp.concatenate([target, target], axis=0).T[0:1, :]
    final_line = jnp.where(iota((1, 128), 1) < 64, diagonal, target_line)
    for i in range(16):
        sent_ref[:, 128 * i : 128 * i + 128] = jnp.broadcast_to(lines[i : i + 1, :], (64, 128))
    sent_ref[:, 2048:2176] = jnp.broadcast_to(final_line, (64, 128))
    spent = jnp.sum(quadratic, axis=0, keepdims=True)
    left_over = rest[3:4, 0:1] - spent[:, 0:1]
    line = iota((8, 128), 0)
    extra_ref[...] = jnp.where(line == 0, left_over, rest[3:4, 1:2])
    logdet_ref[0] = log_sum[0, 0] / COLUMNS


def own_terms(place, parts, own_prior, spectrum, coupling):
    vmem = pl.BlockSpec(memory_space=pltpu.VMEM)
    smem = pl.BlockSpec(memory_space=pltpu.SMEM)
    return pl.pallas_call(
        own_kernel,
        in_specs=[smem] + [vmem] * 7,
        out_specs=[vmem, vmem, smem],
        out_shape=[
            jax.ShapeDtypeStruct((64, WIDTH), f32),
            jax.ShapeDtypeStruct((8, 128), f32),
            jax.ShapeDtypeStruct((1,), f32),
        ],
        scratch_shapes=[pltpu.VMEM((COLUMNS, 384), f32)],
        name="own",
    )(place, *parts, own_prior, spectrum, coupling)


def gradient_kernel(
    place_ref,
    near_ref,
    far_ref,
    coupling_ref,
    spectrum_ref,
    extra_ref,
    coeffs_ref,
    chi_ref,
    flat,
    inverse,
    resid,
    direction,
    mapped,
    answer,
    turned,
):
    for i in range(WIDTH // 128):
        where = slice(128 * i, 128 * i + 128)
        flat[where, :] = jnp.concatenate([near_ref[:, where], far_ref[:, where]], axis=0).T
    line = iota((8, 128), 0)

    def start(r):
        return (r % 16) * 128 + (r // 16) * 64

    def across(c, offset):
        return flat[pl.ds(start(c) + offset, 8, stride=128), :]

    for r in range(32):
        at = start(r)
        corner = flat[2048 + r : 2049 + r, :]
        for c in range(0, 32, 8):
            straight = None if c + 7 < r else flat[at + c : at + c + 8, :]
            crossed = None if c > r else across(c, r)
            if straight is None:
                first = second = crossed
                second = None
            if crossed is None:
                first = straight
            if straight is not None and crossed is not None:
                index = line + c
                first = jnp.where(index > r, straight, crossed)
                first = jnp.where(index == r, corner, first)
            inverse[r, c : c + 8, :] = first
            low = None if c > r else flat[at + c : at + c + 8, :]
            high = None if c + 7 <= r else across(c, r)
            if low is None:
                value = high
            elif high is None:
                value = low
            else:
                value = jnp.where(line + c <= r, low, high)
            inverse[32 + r, 32 + c : 40 + c, :] = value
            inverse[r, 32 + c : 40 + c, :] = flat[at + 32 + c : at + 40 + c, :]
            inverse[32 + r, c : c + 8, :] = across(c, 32 + r)

    row, col = iota((128, 128), 0), iota((128, 128), 1)
    mixing = jnp.where(row == col, 0.0, coupling_ref[...])
    power = power_column(spectrum_ref)
    resid[...] = flat[2112:2176, :]
    direction[...] = jnp.zeros((64, 128), f32)
    mapped[...] = jnp.zeros((64, 128), f32)
    answer[...] = jnp.zeros((64, 128), f32)

    def iterate(_, carry):
        inner, curved = carry
        now = resid[...]
        scaled = jnp.zeros((64, 128), f32)
        for k in range(64):
            scaled = scaled + inverse[k] * resid[k : k + 1, :]
        mixed = jnp.dot(scaled, mixing, precision=highest, preferred_element_type=f32)
        image = now + power * mixed
        old_mapped = mapped[...]
        inner_next = total(now * scaled)
        straight = total(scaled * image)
        crossing = total(scaled * old_mapped)
        ratio = inner_next / inner
        curved = straight + ratio * (2.0 * crossing + ratio * curved)
        step = inner_next / curved
        toward = scaled + ratio * direction[...]
        image = image + ratio * old_mapped
        direction[...] = toward
        mapped[...] = image
        answer[...] = answer[...] + step * toward
        resid[...] = now - step * image
        return inner_next, curved

    lax.fori_loop(0, ITERS, iterate, (jnp.ones((1, 1), f32), jnp.zeros((1, 1), f32)))
    own = place_ref[2]
    value = answer[...]
    gained = jnp.sum(flat[2112:2176, :] * value, axis=0, keepdims=True)
    lane = iota((1, 128), 1)
    gained = jnp.sum(jnp.where(lane == own, gained, 0.0), axis=1, keepdims=True)
    chi = (extra_ref[0:1, 0:1] - gained) / extra_ref[1:2, 0:1]
    chi_ref[0] = chi[0, 0]
    turned[...] = jnp.concatenate([value, value], axis=0).T
    coeffs_ref[...] = turned[pl.ds(own, 1), :][:, 0:64]


def conjugate(place, near, far, coupling, spectrum, extra):
    vmem = pl.BlockSpec(memory_space=pltpu.VMEM)
    smem = pl.BlockSpec(memory_space=pltpu.SMEM)
    square = pltpu.VMEM((64, 128), f32)
    return pl.pallas_call(
        gradient_kernel,
        in_specs=[smem] + [vmem] * 5,
        out_specs=[vmem, smem],
        out_shape=[jax.ShapeDtypeStruct((1, COMMON), f32), jax.ShapeDtypeStruct((1,), f32)],
        scratch_shapes=[
            pltpu.VMEM((WIDTH, 128), f32),
            pltpu.VMEM((64, 64, 128), f32),
            square,
            square,
            square,
            square,
            pltpu.VMEM((128, 128), f32),
        ],
        name="gradient",
    )(place, near, far, coupling, spectrum, extra)


def body(design, noise_weight, residuals, slot_pulsar, slot_rows, own_prior, spectrum, directions):
    toa = lax.axis_index("toa")
    device = lax.axis_index("psr") * lax.axis_size("toa") + toa
    count = lax.axis_size("psr") * lax.axis_size("toa")
    core = toa % 2
    place = jnp.stack([toa // 2, core, device // 2]).astype(jnp.int32)
    spectrum = spectrum.reshape(1, -1)
    mine, other = gram_parts(place, design, noise_weight, residuals, slot_pulsar, slot_rows)
    got = lax.ppermute(other, "toa", [(u, u ^ 1) for u in range(8)])
    parts = [mine[s] + got[s] for s in range(4)]
    for s in range(1, 4):
        parts[s] = lax.ppermute(parts[s], "toa", [(u, (u + 2 * s) % 8) for u in range(8)])
    coupling = coupling_inverse(place, directions)
    sent, extra, log_dets = own_terms(place, parts, own_prior, spectrum, coupling)
    groups = [list(range(c, count, 2)) for c in range(2)]
    near = lax.all_to_all(sent, AXES, 0, 0, tiled=True, axis_index_groups=groups)
    far = lax.ppermute(near, "toa", [(u, u ^ 1) for u in range(8)])
    coeffs, chi_square = conjugate(place, near, far, coupling, spectrum, extra)
    return (coeffs, log_dets, chi_square)


def solution(mesh):
    return jax.shard_map(
        body,
        mesh=mesh,
        in_specs=(
            P(AXES, None, None),
            P(AXES, None),
            P(AXES, None),
            P(AXES),
            P(AXES),
            P(AXES, None),
            P(),
            P(),
        ),
        out_specs=(P(AXES, None), P(AXES), P(AXES)),
        check_vma=False,
    )
```

time: 523 us -> 78.3 us (0.15); the launches traced: 514 us -> 77.9 us
  blocking collectives: 239 us -> 21.2 us
  other arithmetic: 117 us -> 2.46 us
  starting transfers between devices: 73.7 us -> 14.3 us
  between operations: 43.4 us -> 0.9 us
  Pallas kernels: 0 us -> 32.2 us
  matrix products: 24 us -> 0 us
  local copies, waits for them, and re-layouts: 16.8 us -> 3.44 us
    all_gather x8 -> x0, blocking collectives: 239 us -> none  [in_one_piece(): lax.all_gather(both, axis, axis=dim, tiled=True)]
    another operation x21 -> x1, other arithmetic: 83 us -> 0.65 us  [body(): place = jnp.stack([toa // 2, core, device // 2]).astype(jnp.int32)]
    all_to_all x1 -> x0, starting transfers between devices: 73.7 us -> none  [sent_and_summed(): lax.all_to_all(cut_along(value, dim, length), axis, 0, 0, tiled=True)]
    pallas_call x0 -> x4, Pallas kernels: none -> 32.2 us  [the longest x1 13.3 us: own_terms(): pl.pallas_call(own_kernel, in_specs=[smem] + [vmem] * 7, out_specs=[vmem,...]
    reduce_sum x29 -> x0, other arithmetic: 21.5 us -> none  [the longest x8 5.65 us: conjugate_shared(): jnp.sum(curved) + jnp.sum(direction * mixing * inverse_power[None, :])]
    all_to_all x0 -> x1, blocking collectives: none -> 21.2 us  [body(): lax.all_to_all(sent, AXES, 0, 0, tiled=True, axis_index_groups=groups)]
    ppermute x0 -> x5, starting transfers between devices: none -> 14.3 us  [the longest x3 10.2 us: body(): lax.ppermute(parts[s], 'toa', [(u, (u + 2 * s) % 8) for u in range(8)])]
    dot_general x25 -> x0, matrix products: 14.1 us -> none  [the longest x8 6.64 us: conjugate_shared(): jnp.einsum('pcd,pd->pc', schur_part, scaled, precision=highest)]
  transfers between devices with their start and end apart: 1 -> 5, of which waited for: 0 -> 2; matrix products, arithmetic and copies ran while one was open for 5% -> 0% of each run, Pallas kernels for 0% -> 7%
where the time goes in v1:
time: 78.3 us; the launch traced here: 77.9 us
  Pallas kernels  32.2 us (41%)
  blocking collectives  21.2 us (27%)
  starting transfers between devices  14.3 us (18%)
  local copies, waits for them, and re-layouts  3.44 us (4%)
  waiting for transfers between devices  3.36 us (4%)
  other arithmetic  2.46 us (3%)
  between operations  0.9 us (1%)
    all_to_all x1, blocking collectives, body(): lax.all_to_all(sent, AXES, 0, 0, tiled=True, axis_index_groups=groups)  21.2 us
    pallas_call x1, Pallas kernels, own_terms(): pl.pallas_call(own_kernel, in_specs=[smem] + [vmem] * 7, out_specs=[vmem,...  13.3 us
    ppermute x3, starting transfers between devices, body(): lax.ppermute(parts[s], 'toa', [(u, (u + 2 * s) % 8) for u in range(8)])  10.2 us
    pallas_call x1, Pallas kernels, conjugate(): pl.pallas_call(gradient_kernel, in_specs=[smem] + [vmem] * 5, out_specs=[...  6.8 us
    pallas_call x1, Pallas kernels, gram_parts(): pl.pallas_call(gram_kernel, grid_spec=pltpu.PrefetchScalarGridSpec(num_sc...  6.37 us
    pallas_call x1, Pallas kernels, coupling_inverse(): pl.pallas_call(coupling_kernel, in_specs=[pl.BlockSpec(memory_space=pltpu...  5.73 us
    ppermute x1, starting transfers between devices, body(): far = lax.ppermute(near, 'toa', [(u, u ^ 1) for u in range(8)])  2.75 us
    all_to_all x1, local copies, waits for them, and re-layouts, body(): lax.all_to_all(sent, AXES, 0, 0, tiled=True, axis_index_groups=groups)  1.84 us
  transfers between devices with their start and end apart: 5, of which 2 were waited for; matrix products, arithmetic and copies ran while one was open for 0% of the time, Pallas kernels for 7%

profile of v1, /device:TPU:1, one launch (start us, length us, event | category | flops | bytes accessed | tf_op | source)
XLA Modules:
  0.0 77.9 jit_solution(4921891455784892191)
XLA Ops:
  0.7 0.7 pad_add_fusion.place_ref
  1.3 6.4 %gram.1 = (f32[4,264,128]{2,1,0:T(8,128)}, f32[4,264,128]{2,1,0:T(8,128)}) custom-call(s32[96]{0:T(128)} %pulsar_ref.1, s32[96]{0:T(128)} %rows_ref.1, s32[3]{0:T(128)} %pad_add_fusion.place_ref, bf16[96,128,256]{2,1,0:T(8,128)(2,1)} %design_ref.1, f32[96,128]{1,0:T(8,128)} %weight_ref.1, bf16[96,128]{1,0:T(8,128)(2,1)} %resid_ref.1), custom_call_target="tpu_custom_call" | custom-call | tf_op jit(solution)/shard_map/gram/pallas_call | solution.py:189
  7.7 1.4 %collective-permute-start = (f32[4,264,128]{2,1,0:T(8,128)}, f32[4,264,128]{2,1,0:T(8,128)S(1)}, u32[]{:S(2)}, u32[]{:S(2)}) collective-permute-start(f32[4,264,128]{2,1,0:T(8,128)} %get-tuple-element.11), channel_id=1, source_target_pairs={{0,1},{1,0},{2,3},{3,2},{4,5},{5,4},{6,7},{7,6},{8,9},{9,8},{10,11... | collective-permute-start | bytes 1622024 | tf_op jit(solution)/shard_map/ppermute | solution.py:500
  9.1 1.8 %collective-permute-done = f32[4,264,128]{2,1,0:T(8,128)S(1)} collective-permute-done((f32[4,264,128]{2,1,0:T(8,128)}, f32[4,264,128]{2,1,0:T(8,128)S(1)}, u32[]{:S(2)}, u32[]{:S(2)}) %collective-permute-start) | collective-permute-done | bytes 540704 | tf_op jit(solution)/shard_map/ppermute | solution.py:500
  10.8 1.8 %fusion = (f32[264,128]{1,0:T(8,128)S(1)}, f32[264,128]{1,0:T(8,128)S(1)}, f32[264,128]{1,0:T(8,128)S(1)}, f32[264,128]{1,0:T(8,128)}) fusion(f32[4,264,128]{2,1,0:T(8,128)S(1)} %collective-permute-done, f32[4,264,128]{2,1,0:T(8,128)} %get-tuple-element.10), kind=kLoop, calls=%fused_computation.2 | loop fusion | flops 135168 | bytes 1622016 | tf_op jit(solution)/shard_map/add | solution.py:501
  12.7 6.3 %collective-permute-start.1 = (f32[264,128]{1,0:T(8,128)S(1)}, f32[264,128]{1,0:T(8,128)S(1)}, u32[]{:S(2)}, u32[]{:S(2)}) collective-permute-start(f32[264,128]{1,0:T(8,128)S(1)} %get-tuple-element.19), channel_id=1, source_target_pairs={{0,2},{1,3},{2,4},{3,5},{4,6},{5,7},{6,0},{7,1},{8,10},{9,11},{10,... | collective-permute-start | bytes 405512 | tf_op jit(solution)/shard_map/ppermute | solution.py:503
  19.0 2.9 %collective-permute-start.2 = (f32[264,128]{1,0:T(8,128)S(1)}, f32[264,128]{1,0:T(8,128)S(1)}, u32[]{:S(2)}, u32[]{:S(2)}) collective-permute-start(f32[264,128]{1,0:T(8,128)S(1)} %get-tuple-element.18), channel_id=1, source_target_pairs={{0,4},{1,5},{2,6},{3,7},{4,0},{5,1},{6,2},{7,3},{8,12},{9,13},{10,... | collective-permute-start | bytes 405512 | tf_op jit(solution)/shard_map/ppermute | solution.py:503
  21.9 1.0 %collective-permute-start.3 = (f32[264,128]{1,0:T(8,128)S(1)}, f32[264,128]{1,0:T(8,128)S(1)}, u32[]{:S(2)}, u32[]{:S(2)}) collective-permute-start(f32[264,128]{1,0:T(8,128)S(1)} %get-tuple-element.17), channel_id=1, source_target_pairs={{0,6},{1,7},{2,0},{3,1},{4,2},{5,3},{6,4},{7,5},{8,14},{9,15},{10,... | collective-permute-start | bytes 405512 | tf_op jit(solution)/shard_map/ppermute | solution.py:503
  22.9 5.7 %coupling.1.coupling_ref = f32[128,128]{1,0:T(8,128)} custom-call(s32[3]{0:T(128)} %pad_add_fusion.place_ref, f32[3,128]{1,0:T(4,128)} %directions_ref.1), custom_call_target="tpu_custom_call" | custom-call | tf_op jit(solution)/shard_map/coupling/pallas_call | solution.py:239
  28.6 0.0 collective-permute-done.1.part1
  28.6 0.0 collective-permute-done.2.part2
  28.6 0.0 copy-start.3
  28.6 0.0 collective-permute-done.3.part3
  28.6 0.0 copy-start.4
  28.6 0.6 copy-done.2
  29.3 0.0 copy-done.3
  29.3 0.1 copy-done.4
  29.4 13.3 %own.1 = (f32[64,2176]{1,0:T(8,128)}, f32[8,128]{1,0:T(8,128)}, f32[1]{0:T(128)}) custom-call(s32[3]{0:T(128)} %pad_add_fusion.place_ref, f32[264,128]{1,0:T(8,128)} %get-tuple-element.20.part0, f32[264,128]{1,0:T(8,128)} %copy-done.2, f32[264,128]{1,0:T(8,128)} %copy-done.3, f32[264,128]{1,0:T(8,128)} %copy-done.4, f32[1,192]{1,0:T(1,128)} %prior_ref.1, ...), custom_call_target="tpu_custom_call" | custom-call | tf_op jit(solution)/shard_map/own/pallas_call | solution.py:357
  42.7 1.8 %copy.11 = f32[64,1,2176]{2,1,0:T(1,128)S(1)} copy(f32[64,1,2176]{2,0,1:T(8,128)} %bitcast.18) | data formatting | bytes 1114112 | tf_op jit(solution)/shard_map/all_to_all | solution.py:507
  44.5 21.2 %all_to_all.11 = f32[64,1,2176]{2,1,0:T(1,128)S(1)} all-to-all(f32[64,1,2176]{2,1,0:T(1,128)S(1)} %copy.11), channel_id=1, replica_groups={{0,2,4,6,8,10,12,14,16,18,20,22,24,26,28,30,32,34,36,38,40,42,44,46,48,..., dimensions={0} | all-to-all | bytes 1114112 | tf_op jit(solution)/shard_map/all_to_all | solution.py:507
  65.8 2.7 %collective-permute-start.4 = (f32[64,2176]{1,0:T(8,128)S(1)}, f32[64,2176]{1,0:T(8,128)S(1)}, u32[]{:S(2)}, u32[]{:S(2)}) collective-permute-start(f32[64,2176]{1,0:T(8,128)S(1)} %bitcast.16), channel_id=1, source_target_pairs={{0,1},{1,0},{2,3},{3,2},{4,5},{5,4},{6,7},{7,6},{8,9},{9,8},{10,11... | collective-permute-start | bytes 1671176 | tf_op jit(solution)/shard_map/ppermute | solution.py:508
  68.5 1.6 %collective-permute-done.4.far_ref = f32[64,2176]{1,0:T(8,128)S(1)} collective-permute-done((f32[64,2176]{1,0:T(8,128)S(1)}, f32[64,2176]{1,0:T(8,128)S(1)}, u32[]{:S(2)}, u32[]{:S(2)}) %collective-permute-start.4) | collective-permute-done | bytes 557088 | tf_op jit(solution)/shard_map/ppermute | solution.py:508
  70.1 0.8 %copy-done.1 = f32[64,2176]{1,0:T(8,128)} copy-done((f32[64,2176]{1,0:T(8,128)}, f32[64,2176]{1,0:T(8,128)S(1)}, u32[]{:S(2)}) %copy-start.1) | copy-done | bytes 557080
  70.9 6.8 %gradient.1 = (f32[1,64]{1,0:T(1,128)}, f32[1]{0:T(128)}) custom-call(s32[3]{0:T(128)} %pad_add_fusion.place_ref, f32[64,2176]{1,0:T(8,128)} %bitcast.17, f32[64,2176]{1,0:T(8,128)} %copy-done.1, f32[128,128]{1,0:T(8,128)} %coupling.1.coupling_ref, f32[1,32]{1,0:T(1,128)} %bitcast.20, f32[8,128]{1,0:T(8,128)} %get-tuple-element.13.extra_ref), custom_call_target="tpu_custom_call" | custom-call | tf_op jit(solution)/shard_map/gradient/pallas_call | solution.py:474
  (5 shorter events, 0.0 us)
Async XLA Ops:
  7.7 3.2 %collective-permute-start = (f32[4,264,128]{2,1,0:T(8,128)}, f32[4,264,128]{2,1,0:T(8,128)S(1)}, u32[]{:S(2)}, u32[]{:S(2)}) collective-permute-start(f32[4,264,128]{2,1,0:T(8,128)} %get-tuple-element.11), channel_id=1, source_target_pairs={{0,1},{1,0},{2,3},{3,2},{4,5},{5,4},{6,7},{7,6},{8,9},{9,8},{10,11... | collective-permute-start | bytes 1622024 | tf_op jit(solution)/shard_map/ppermute | solution.py:500
  12.7 16.0 %collective-permute-start.1 = (f32[264,128]{1,0:T(8,128)S(1)}, f32[264,128]{1,0:T(8,128)S(1)}, u32[]{:S(2)}, u32[]{:S(2)}) collective-permute-start(f32[264,128]{1,0:T(8,128)S(1)} %get-tuple-element.19), channel_id=1, source_target_pairs={{0,2},{1,3},{2,4},{3,5},{4,6},{5,7},{6,0},{7,1},{8,10},{9,11},{10,... | collective-permute-start | bytes 405512 | tf_op jit(solution)/shard_map/ppermute | solution.py:503
  19.0 9.6 %collective-permute-start.2 = (f32[264,128]{1,0:T(8,128)S(1)}, f32[264,128]{1,0:T(8,128)S(1)}, u32[]{:S(2)}, u32[]{:S(2)}) collective-permute-start(f32[264,128]{1,0:T(8,128)S(1)} %get-tuple-element.18), channel_id=1, source_target_pairs={{0,4},{1,5},{2,6},{3,7},{4,0},{5,1},{6,2},{7,3},{8,12},{9,13},{10,... | collective-permute-start | bytes 405512 | tf_op jit(solution)/shard_map/ppermute | solution.py:503
  21.9 6.8 %collective-permute-start.3 = (f32[264,128]{1,0:T(8,128)S(1)}, f32[264,128]{1,0:T(8,128)S(1)}, u32[]{:S(2)}, u32[]{:S(2)}) collective-permute-start(f32[264,128]{1,0:T(8,128)S(1)} %get-tuple-element.17), channel_id=1, source_target_pairs={{0,6},{1,7},{2,0},{3,1},{4,2},{5,3},{6,4},{7,5},{8,14},{9,15},{10,... | collective-permute-start | bytes 405512 | tf_op jit(solution)/shard_map/ppermute | solution.py:503
  28.6 0.7 copy-start.2
  28.6 0.7 copy-start.3
  28.6 0.7 copy-start.4
  65.8 4.3 %copy-start = (f32[64,1,2176]{2,0,1:T(8,128)}, f32[64,1,2176]{2,0,1:T(8,128)S(1)}, u32[]{:S(2)}) copy-start(f32[64,1,2176]{2,0,1:T(8,128)S(1)} %copy.14) | copy-start | bytes 1671172
  65.8 4.3 %collective-permute-start.4 = (f32[64,2176]{1,0:T(8,128)S(1)}, f32[64,2176]{1,0:T(8,128)S(1)}, u32[]{:S(2)}, u32[]{:S(2)}) collective-permute-start(f32[64,2176]{1,0:T(8,128)S(1)} %bitcast.16), channel_id=1, source_target_pairs={{0,1},{1,0},{2,3},{3,2},{4,5},{5,4},{6,7},{7,6},{8,9},{9,8},{10,11... | collective-permute-start | bytes 1671176 | tf_op jit(solution)/shard_map/ppermute | solution.py:508
  70.1 0.8 %copy-start.1 = (f32[64,2176]{1,0:T(8,128)}, f32[64,2176]{1,0:T(8,128)S(1)}, u32[]{:S(2)}) copy-start(f32[64,2176]{1,0:T(8,128)S(1)} %collective-permute-done.4.far_ref) | copy-start | bytes 1671172

commit v2 on v1

--- a/solution.py
+++ b/solution.py
@@ -9,13 +9,18 @@
 ITERS = 8
 COLUMNS = 256
 COMMON = 64
-STEP_BLOCKS = 16
+STEP_BLOCKS = 8
 ROWS_SENT = 264
 WIDTH = 2176
+LINES = WIDTH // 128
 AXES = ("psr", "toa")
 
 highest = lax.Precision.HIGHEST
 f32 = jnp.float32
+
+
+def in_vmem(value):
+    return pltpu.with_memory_space_constraint(value, pltpu.VMEM)
 
 
 def iota(shape, dim):
@@ -81,130 +86,130 @@
     resid_ref,
     mine_ref,
     other_ref,
+    blocks,
     gram,
     fit,
     energy,
     wide_resid,
     counts,
+    arrived,
 ):
-    step = pl.program_id(0)
-
-    @pl.when(step == 0)
-    def _():
-        gram[...] = jnp.zeros(gram.shape, f32)
-        fit[...] = jnp.zeros(fit.shape, f32)
-        energy[...] = jnp.zeros(energy.shape, f32)
-        for k in range(GROUP_PULSARS):
-            counts[k] = 0
-
+    slots = weight_ref.shape[0]
+    steps = slots // STEP_BLOCKS
+
+    def load(step):
+        where = pl.ds(step * STEP_BLOCKS, STEP_BLOCKS)
+        return pltpu.make_async_copy(design_ref.at[where], blocks.at[where], arrived.at[step])
+
+    for step in range(steps):
+        load(step).start()
+    gram[...] = jnp.zeros(gram.shape, f32)
+    fit[...] = jnp.zeros(fit.shape, f32)
+    energy[...] = jnp.zeros(energy.shape, f32)
+    for k in range(GROUP_PULSARS):
+        counts[k] = 0
     wide_resid[...] = resid_ref[...].astype(f32)
     lane = iota((1, 128), 1)
 
-    def add_blocks(local, number, pulsar):
-        pieces, fitted, squares = [], None, None
-        for i in range(number):
-            valid = rows_ref[step * STEP_BLOCKS + local + i]
-            weight = jnp.where(lane < valid, weight_ref[pl.ds(local + i, 1), :], 0.0)
-            resid = wide_resid[pl.ds(local + i, 1), :]
-            turned = design_ref[local + i].T.astype(f32)
-            weighted = (turned * weight).astype(jnp.bfloat16)
-            pieces.append(weighted)
-            product = weighted.astype(f32) * resid
-            square = weight * resid * resid
-            fitted = product if fitted is None else fitted + product
-            squares = square if squares is None else squares + square
-            counts[pulsar] = counts[pulsar] + valid
-        left = jnp.concatenate(pieces, axis=1) if number > 1 else pieces[0]
-        right = design_ref[pl.ds(local, number)].reshape(number * 128, COLUMNS)
-        gram[pulsar] = gram[pulsar] + jnp.dot(left, right, preferred_element_type=f32)
-        fit[pulsar] = fit[pulsar] + fitted
-        energy[pl.ds(pulsar, 1), :] = energy[pl.ds(pulsar, 1), :] + squares
-
-    def quad(q, carry):
-        at = step * STEP_BLOCKS + q * 4
-        pulsars = [pulsar_ref[at + i] for i in range(4)]
-        filled = rows_ref[at] + rows_ref[at + 1] + rows_ref[at + 2] + rows_ref[at + 3] > 0
-        same = (
-            (pulsars[0] == pulsars[1])
-            & (pulsars[1] == pulsars[2])
-            & (pulsars[2] == pulsars[3])
-        )
-
-        @pl.when(filled & same)
+    def one_step(step, carry):
+        load(step).wait()
+        at = step * STEP_BLOCKS
+        pulsars = [pulsar_ref[at + i] for i in range(STEP_BLOCKS)]
+        rows = [rows_ref[at + i] for i in range(STEP_BLOCKS)]
+        same = pulsars[1] == pulsars[0]
+        for i in range(2, STEP_BLOCKS):
+            same = same & (pulsars[i] == pulsars[0])
+        low = jnp.where(same, pulsars[0], 0)
+        high = jnp.where(same, pulsars[0] + 1, GROUP_PULSARS)
+
+        def one_pulsar(pulsar, carry):
+            valid = [jnp.where(pulsars[i] == pulsar, rows[i], 0) for i in range(STEP_BLOCKS)]
+            number = valid[0]
+            for i in range(1, STEP_BLOCKS):
+                number = number + valid[i]
+
+            @pl.when(number > 0)
+            def _():
+                pieces, fitted, squares = [], None, None
+                for i in range(STEP_BLOCKS):
+                    weight = jnp.where(lane < valid[i], weight_ref[pl.ds(at + i, 1), :], 0.0)
+                    resid = wide_resid[pl.ds(at + i, 1), :]
+                    turned = blocks[at + i].T.astype(f32)
+                    weighted = (turned * weight).astype(jnp.bfloat16)
+                    pieces.append(weighted)
+                    product = weighted.astype(f32) * resid
+                    square = weight * resid * resid
+                    fitted = product if fitted is None else fitted + product
+                    squares = square if squares is None else squares + square
+                left = jnp.concatenate(pieces, axis=1)
+                right = blocks[pl.ds(at, STEP_BLOCKS)].reshape(STEP_BLOCKS * 128, COLUMNS)
+                gram[pulsar] = gram[pulsar] + jnp.dot(left, right, preferred_element_type=f32)
+                fit[pulsar] = fit[pulsar] + fitted
+                energy[pl.ds(pulsar, 1), :] = energy[pl.ds(pulsar, 1), :] + squares
+                counts[pulsar] = counts[pulsar] + number
+
+            return carry
+
+        return lax.fori_loop(low, high, one_pulsar, carry)
+
+    lax.fori_loop(0, steps, one_step, 0)
+
+    row, col = iota((128, 128), 0), iota((128, 128), 1)
+    line = iota((8, 128), 0)
+    spot = iota((8, 128), 1)
+    height = place_ref[0]
+    core = place_ref[1]
+
+    def pack(out_ref, s, k):
+        @pl.when(counts[k] == 0)
         def _():
-            add_blocks(q * 4, 4, pulsars[0])
-
-        @pl.when(filled & jnp.logical_not(same))
+            out_ref[s] = jnp.zeros((ROWS_SENT, 128), f32)
+
+        @pl.when(counts[k] > 0)
         def _():
-            for i in range(4):
-                add_blocks(q * 4 + i, 1, pulsars[i])
-
-        return carry
-
-    lax.fori_loop(0, STEP_BLOCKS // 4, quad, 0)
-
-    @pl.when(step == pl.num_programs(0) - 1)
-    def _():
-        row, col = iota((128, 128), 0), iota((128, 128), 1)
-        line = iota((8, 128), 0)
-        spot = iota((8, 128), 1)
-
-        def pack(out_ref, s, k):
-            @pl.when(counts[k] == 0)
-            def _():
-                out_ref[s] = jnp.zeros((ROWS_SENT, 128), f32)
-
-            @pl.when(counts[k] > 0)
-            def _():
-                upper = gram[k, 0:128, 0:128]
-                lower = gram[k, 128:256, 128:256]
-                upper = 0.5 * (upper + upper.T)
-                lower = 0.5 * (lower + lower.T)
-                cross = 0.5 * (gram[k, 128:256, 0:128] + gram[k, 0:128, 128:256].T)
-                out_ref[s, 0:128, :] = jnp.where(col > row, upper, lower)
-                out_ref[s, 128:256, :] = cross
-                diagonal = jnp.sum(jnp.where(col == row, upper, 0.0), axis=0, keepdims=True)
-                first = jnp.sum(fit[k, 0:128, :].T, axis=0, keepdims=True)
-                second = jnp.sum(fit[k, 128:256, :].T, axis=0, keepdims=True)
-                power = jnp.sum(energy[pl.ds(k, 1), :], axis=1, keepdims=True)
-                number = counts[k].astype(f32)
-                last = jnp.where(spot == 0, power, jnp.where(spot == 1, number, 0.0))
-                rest = jnp.where(line == 3, last, 0.0)
-                rest = jnp.where(line == 0, diagonal, rest)
-                rest = jnp.where(line == 1, first, rest)
-                out_ref[s, 256:264, :] = jnp.where(line == 2, second, rest)
-
-        height = place_ref[0]
-        core = place_ref[1]
-        for s in range(4):
-            base = 2 * ((height + s) & 3)
-            pack(mine_ref, s, base + core)
-            pack(other_ref, s, base + 1 - core)
+            upper = gram[k, 0:128, 0:128]
+            lower = gram[k, 128:256, 128:256]
+            upper = 0.5 * (upper + upper.T)
+            lower = 0.5 * (lower + lower.T)
+            cross = 0.5 * (gram[k, 128:256, 0:128] + gram[k, 0:128, 128:256].T)
+            out_ref[s, 0:128, :] = jnp.where(col > row, upper, lower)
+            out_ref[s, 128:256, :] = cross
+            diagonal = jnp.sum(jnp.where(col == row, upper, 0.0), axis=0, keepdims=True)
+            first = jnp.sum(fit[k, 0:128, :].T, axis=0, keepdims=True)
+            second = jnp.sum(fit[k, 128:256, :].T, axis=0, keepdims=True)
+            power = jnp.sum(energy[pl.ds(k, 1), :], axis=1, keepdims=True)
+            number = counts[k].astype(f32)
+            last = jnp.where(spot == 0, power, jnp.where(spot == 1, number, 0.0))
+            rest = jnp.where(line == 3, last, 0.0)
+            rest = jnp.where(line == 0, diagonal, rest)
+            rest = jnp.where(line == 1, first, rest)
+            out_ref[s, 256:264, :] = jnp.where(line == 2, second, rest)
+
+    for s in range(4):
+        base = 2 * ((height + s) & 3)
+        pack(other_ref, s, base + 1 - core)
+        pack(mine_ref, s, base + core)
 
 
 def gram_parts(place, design, weight, residuals, slot_pulsar, slot_rows):
     slots = design.shape[0]
-    piece = jax.ShapeDtypeStruct((4, ROWS_SENT, 128), f32)
-    whole = pl.BlockSpec((4, ROWS_SENT, 128), lambda i, *_: (0, 0, 0))
+    piece = pltpu.VMEM((4, ROWS_SENT, 128), f32)
+    smem = pl.BlockSpec(memory_space=pltpu.SMEM)
+    vmem = pl.BlockSpec(memory_space=pltpu.VMEM)
+    hbm = pl.BlockSpec(memory_space=pl.ANY)
     return pl.pallas_call(
         gram_kernel,
-        grid_spec=pltpu.PrefetchScalarGridSpec(
-            num_scalar_prefetch=3,
-            grid=(slots // STEP_BLOCKS,),
-            in_specs=[
-                pl.BlockSpec((STEP_BLOCKS, 128, COLUMNS), lambda i, *_: (i, 0, 0)),
-                pl.BlockSpec((STEP_BLOCKS, 128), lambda i, *_: (i, 0)),
-                pl.BlockSpec((STEP_BLOCKS, 128), lambda i, *_: (i, 0)),
-            ],
-            out_specs=[whole, whole],
-            scratch_shapes=[
-                pltpu.VMEM((GROUP_PULSARS, COLUMNS, COLUMNS), f32),
-                pltpu.VMEM((GROUP_PULSARS, COLUMNS, 128), f32),
-                pltpu.VMEM((GROUP_PULSARS, 128), f32),
-                pltpu.VMEM((STEP_BLOCKS, 128), f32),
-                pltpu.SMEM((GROUP_PULSARS,), jnp.int32),
-            ],
-        ),
+        in_specs=[smem, smem, smem, hbm, vmem, vmem],
+        out_specs=[vmem, vmem],
+        scratch_shapes=[
+            pltpu.VMEM((slots, 128, COLUMNS), jnp.bfloat16),
+            pltpu.VMEM((GROUP_PULSARS, COLUMNS, COLUMNS), f32),
+            pltpu.VMEM((GROUP_PULSARS, COLUMNS, 128), f32),
+            pltpu.VMEM((GROUP_PULSARS, 128), f32),
+            pltpu.VMEM((slots, 128), f32),
+            pltpu.SMEM((GROUP_PULSARS,), jnp.int32),
+            pltpu.SemaphoreType.DMA((slots // STEP_BLOCKS,)),
+        ],
         out_shape=[piece, piece],
         name="gram",
     )(slot_pulsar, slot_rows, place, design, weight, residuals)
@@ -243,7 +248,7 @@
             pl.BlockSpec(memory_space=pltpu.VMEM),
         ],
         out_specs=pl.BlockSpec(memory_space=pltpu.VMEM),
-        out_shape=jax.ShapeDtypeStruct((128, 128), f32),
+        out_shape=pltpu.VMEM((128, 128), f32),
         name="coupling",
     )(place, directions)
 
@@ -257,6 +262,7 @@
 
 def own_kernel(
     place_ref,
+    kept,
     part0,
     part1,
     part2,
@@ -272,7 +278,8 @@
     row, col = iota((128, 128), 0), iota((128, 128), 1)
 
     def summed(lo, hi):
-        return (part0[lo:hi, :] + part1[lo:hi, :]) + (part2[lo:hi, :] + part3[lo:hi, :])
+        near = kept[0, lo:hi, :] + part0[0, lo:hi, :]
+        return (near + part1[lo:hi, :]) + (part2[lo:hi, :] + part3[lo:hi, :])
 
     packed = summed(0, 128)
     cross = summed(128, 256)
@@ -341,9 +348,10 @@
     target = work[0:64, 256:384]
     target_line = jnp.concatenate([target, target], axis=0).T[0:1, :]
     final_line = jnp.where(iota((1, 128), 1) < 64, diagonal, target_line)
-    for i in range(16):
-        sent_ref[:, 128 * i : 128 * i + 128] = jnp.broadcast_to(lines[i : i + 1, :], (64, 128))
-    sent_ref[:, 2048:2176] = jnp.broadcast_to(final_line, (64, 128))
+    whole = jnp.concatenate([lines, final_line], axis=0)
+    whole = jnp.concatenate([whole] * 8, axis=0)
+    for i in range(8):
+        sent_ref[8 * LINES * i : 8 * LINES * (i + 1), :] = whole
     spent = jnp.sum(quadratic, axis=0, keepdims=True)
     left_over = rest[3:4, 0:1] - spent[:, 0:1]
     line = iota((8, 128), 0)
@@ -356,16 +364,16 @@
     smem = pl.BlockSpec(memory_space=pltpu.SMEM)
     return pl.pallas_call(
         own_kernel,
-        in_specs=[smem] + [vmem] * 7,
+        in_specs=[smem] + [vmem] * 8,
         out_specs=[vmem, vmem, smem],
         out_shape=[
-            jax.ShapeDtypeStruct((64, WIDTH), f32),
-            jax.ShapeDtypeStruct((8, 128), f32),
+            pltpu.VMEM((64 * LINES, 128), f32),
+            pltpu.VMEM((8, 128), f32),
             jax.ShapeDtypeStruct((1,), f32),
         ],
         scratch_shapes=[pltpu.VMEM((COLUMNS, 384), f32)],
         name="own",
-    )(place, *parts, own_prior, spectrum, coupling)
+    )(place, *map(in_vmem, parts), own_prior, spectrum, in_vmem(coupling))
 
 
 def gradient_kernel(
@@ -385,9 +393,10 @@
     answer,
     turned,
 ):
-    for i in range(WIDTH // 128):
+    for i in range(LINES):
         where = slice(128 * i, 128 * i + 128)
-        flat[where, :] = jnp.concatenate([near_ref[:, where], far_ref[:, where]], axis=0).T
+        rows = pl.ds(i, 64, stride=LINES)
+        flat[where, :] = jnp.concatenate([near_ref[rows, :], far_ref[rows, :]], axis=0).T
     line = iota((8, 128), 0)
 
     def start(r):
@@ -486,7 +495,7 @@
             pltpu.VMEM((128, 128), f32),
         ],
         name="gradient",
-    )(place, near, far, coupling, spectrum, extra)
+    )(place, in_vmem(near), in_vmem(far), in_vmem(coupling), spectrum, in_vmem(extra))
 
 
 def body(design, noise_weight, residuals, slot_pulsar, slot_rows, own_prior, spectrum, directions):
@@ -498,13 +507,16 @@
     spectrum = spectrum.reshape(1, -1)
     mine, other = gram_parts(place, design, noise_weight, residuals, slot_pulsar, slot_rows)
     got = lax.ppermute(other, "toa", [(u, u ^ 1) for u in range(8)])
-    parts = [mine[s] + got[s] for s in range(4)]
+    parts = [mine, got]
     for s in range(1, 4):
-        parts[s] = lax.ppermute(parts[s], "toa", [(u, (u + 2 * s) % 8) for u in range(8)])
+        part = mine[s] + got[s]
+        parts.append(lax.ppermute(part, "toa", [(u, (u + 2 * s) % 8) for u in range(8)]))
     coupling = coupling_inverse(place, directions)
     sent, extra, log_dets = own_terms(place, parts, own_prior, spectrum, coupling)
     groups = [list(range(c, count, 2)) for c in range(2)]
+    sent = sent.reshape(64, 1, WIDTH)
     near = lax.all_to_all(sent, AXES, 0, 0, tiled=True, axis_index_groups=groups)
+    near = near.reshape(64 * LINES, 128)
     far = lax.ppermute(near, "toa", [(u, u ^ 1) for u in range(8)])
     coeffs, chi_square = conjugate(place, near, far, coupling, spectrum, extra)
     return (coeffs, log_dets, chi_square)

time: 78.3 us -> 69.2 us (0.88)
  starting transfers between devices: 14.3 us -> 8.39 us
  waiting for transfers between devices: 3.36 us -> 6.89 us
  local copies, waits for them, and re-layouts: 3.44 us -> 0 us
  other arithmetic: 2.46 us -> 0.7 us
  Pallas kernels: 32.2 us -> 31.3 us
    ppermute x3, starting transfers between devices: 10.2 us -> 5.65 us  [body(): lax.ppermute(part, 'toa', [(u, (u + 2 * s) % 8) for u in range(8)])]
    ppermute x3, waiting for transfers between devices: 0.01 us -> 3.38 us  [body(): lax.ppermute(part, 'toa', [(u, (u + 2 * s) % 8) for u in range(8)])]
    all_to_all x1 -> x0, local copies, waits for them, and re-layouts: 1.84 us -> none  [body(): lax.all_to_all(sent, AXES, 0, 0, tiled=True, axis_index_groups=groups)]
    add x1, other arithmetic: 1.81 us -> 0.04 us  [body(): part = mine[s] + got[s]]
    unnamed x11 -> x0, local copies, waits for them, and re-layouts: 1.6 us -> none
    ppermute x1, starting transfers between devices: 1.38 us -> 0.09 us  [body(): got = lax.ppermute(other, 'toa', [(u, u ^ 1) for u in range(8)])]
  transfers between devices with their start and end apart: 5 -> 5, of which waited for: 2 -> 3; matrix products, arithmetic and copies ran while one was open for 0% -> 0% of each run, Pallas kernels for 7% -> 7%
where the time goes in v2:
time: 69.2 us; the launch traced here: 68.9 us
  Pallas kernels  31.3 us (45%)
  blocking collectives  20.8 us (30%)
  starting transfers between devices  8.39 us (12%)
  waiting for transfers between devices  6.89 us (10%)
  between operations  0.87 us (1%)
  other arithmetic  0.7 us (1%)
    all_to_all x1, blocking collectives, body(): lax.all_to_all(sent, AXES, 0, 0, tiled=True, axis_index_groups=groups)  20.8 us
    pallas_call x1, Pallas kernels, own_terms(): pl.pallas_call(own_kernel, in_specs=[smem] + [vmem] * 8, out_specs=[vmem,...  12.5 us
    pallas_call x1, Pallas kernels, gram_parts(): pl.pallas_call(gram_kernel, in_specs=[smem, smem, smem, hbm, vmem, vmem],...  7.41 us
    pallas_call x1, Pallas kernels, conjugate(): pl.pallas_call(gradient_kernel, in_specs=[smem] + [vmem] * 5, out_specs=[...  6.27 us
    ppermute x3, starting transfers between devices, body(): lax.ppermute(part, 'toa', [(u, (u + 2 * s) % 8) for u in range(8)])  5.65 us
    pallas_call x1, Pallas kernels, coupling_inverse(): pl.pallas_call(coupling_kernel, in_specs=[pl.BlockSpec(memory_space=pltpu...  5.12 us
    ppermute x3, waiting for transfers between devices, body(): lax.ppermute(part, 'toa', [(u, (u + 2 * s) % 8) for u in range(8)])  3.38 us
    ppermute x1, starting transfers between devices, body(): far = lax.ppermute(near, 'toa', [(u, u ^ 1) for u in range(8)])  2.66 us
  transfers between devices with their start and end apart: 5, of which 3 were waited for; matrix products, arithmetic and copies ran while one was open for 0% of the time, Pallas kernels for 7%

profile of v2, /device:TPU:1, one launch (start us, length us, event | category | flops | bytes accessed | tf_op | source)
XLA Modules:
  0.0 68.9 jit_solution(17669097795555085787)
XLA Ops:
  0.7 0.7 pad_add_fusion.place_ref
  1.3 7.4 %gram.1 = (f32[4,264,128]{2,1,0:T(8,128)S(1)}, f32[4,264,128]{2,1,0:T(8,128)S(1)}) custom-call(s32[96]{0:T(128)} %pulsar_ref.1, s32[96]{0:T(128)} %rows_ref.1, s32[3]{0:T(128)} %pad_add_fusion.place_ref, bf16[96,128,256]{2,1,0:T(8,128)(2,1)} %design_ref.1, f32[96,128]{1,0:T(8,128)} %weight_ref.1, bf16[96,128]{1,0:T(8,128)(2,1)} %resid_ref.1), custom_call_target="tpu_custom_call" | custom-call | tf_op jit(solution)/shard_map/gram/pallas_call | solution.py:200
  8.7 0.1 collective-permute-start
  8.8 1.9 %collective-permute-done.part0 = f32[4,264,128]{2,1,0:T(8,128)S(1)} collective-permute-done((f32[4,264,128]{2,1,0:T(8,128)S(1)}, f32[4,264,128]{2,1,0:T(8,128)S(1)}, u32[]{:S(2)}, u32[]{:S(2)}) %collective-permute-start) | collective-permute-done | bytes 540704 | tf_op jit(solution)/shard_map/ppermute | solution.py:509
  10.8 4.3 %collective-permute-start.3 = (f32[264,128]{1,0:T(8,128)S(1)}, f32[264,128]{1,0:T(8,128)S(1)}, u32[]{:S(2)}, u32[]{:S(2)}) collective-permute-start(f32[264,128]{1,0:T(8,128)S(1)} %get-tuple-element.17), channel_id=1, source_target_pairs={{0,6},{1,7},{2,0},{3,1},{4,2},{5,3},{6,4},{7,5},{8,14},{9,15},{10,... | collective-permute-start | bytes 405512 | tf_op jit(solution)/shard_map/ppermute | solution.py:513
  15.0 1.1 %collective-permute-start.2 = (f32[264,128]{1,0:T(8,128)S(1)}, f32[264,128]{1,0:T(8,128)S(1)}, u32[]{:S(2)}, u32[]{:S(2)}) collective-permute-start(f32[264,128]{1,0:T(8,128)S(1)} %get-tuple-element.18), channel_id=1, source_target_pairs={{0,4},{1,5},{2,6},{3,7},{4,0},{5,1},{6,2},{7,3},{8,12},{9,13},{10,... | collective-permute-start | bytes 405512 | tf_op jit(solution)/shard_map/ppermute | solution.py:513
  16.1 0.3 collective-permute-start.1
  16.4 5.1 %coupling.1.coupling_ref = f32[128,128]{1,0:T(8,128)S(1)} custom-call(s32[3]{0:T(128)} %pad_add_fusion.place_ref, f32[3,128]{1,0:T(4,128)} %directions_ref.1), custom_call_target="tpu_custom_call" | custom-call | tf_op jit(solution)/shard_map/coupling/pallas_call | solution.py:244
  21.6 0.0 collective-permute-done.3.part3
  21.6 0.0 collective-permute-done.2.part2
  21.6 3.4 %collective-permute-done.1.part1 = f32[264,128]{1,0:T(8,128)S(1)} collective-permute-done((f32[264,128]{1,0:T(8,128)S(1)}, f32[264,128]{1,0:T(8,128)S(1)}, u32[]{:S(2)}, u32[]{:S(2)}) %collective-permute-start.1) | collective-permute-done | bytes 135200 | tf_op jit(solution)/shard_map/ppermute | solution.py:513
  25.0 12.5 %own.1 = (f32[1088,128]{1,0:T(8,128)S(1)}, f32[8,128]{1,0:T(8,128)S(1)}, f32[1]{0:T(128)}) custom-call(s32[3]{0:T(128)} %pad_add_fusion.place_ref, f32[4,264,128]{2,1,0:T(8,128)S(1)} %get-tuple-element.10.kept, f32[4,264,128]{2,1,0:T(8,128)S(1)} %collective-permute-done.part0, f32[264,128]{1,0:T(8,128)S(1)} %collective-permute-done.1.part1, ...), custom_call_target="tpu_custom_call" | custom-call | tf_op jit(solution)/shard_map/own/pallas_call | solution.py:365
  37.5 20.8 %all_to_all.5 = f32[64,1,2176]{2,1,0:T(1,128)S(1)} all-to-all(f32[64,1,2176]{2,1,0:T(1,128)S(1)} %bitcast.14), channel_id=1, replica_groups={{0,2,4,6,8,10,12,14,16,18,20,22,24,26,28,30,32,34,36,38,40,42,44,46,48,..., dimensions={0} | all-to-all | bytes 1114112 | tf_op jit(solution)/shard_map/all_to_all | solution.py:518
  58.2 2.7 %collective-permute-start.4 = (f32[1088,128]{1,0:T(8,128)S(1)}, f32[1088,128]{1,0:T(8,128)S(1)}, u32[]{:S(2)}, u32[]{:S(2)}) collective-permute-start(f32[1088,128]{1,0:T(8,128)S(1)} %bitcast.12), channel_id=1, source_target_pairs={{0,1},{1,0},{2,3},{3,2},{4,5},{5,4},{6,7},{7,6},{8,9},{9,8},{10,11... | collective-permute-start | bytes 1671176 | tf_op jit(solution)/shard_map/ppermute | solution.py:520
  60.9 1.6 %collective-permute-done.4.far_ref = f32[1088,128]{1,0:T(8,128)S(1)} collective-permute-done((f32[1088,128]{1,0:T(8,128)S(1)}, f32[1088,128]{1,0:T(8,128)S(1)}, u32[]{:S(2)}, u32[]{:S(2)}) %collective-permute-start.4) | collective-permute-done | bytes 557088 | tf_op jit(solution)/shard_map/ppermute | solution.py:520
  62.5 6.3 %gradient.1 = (f32[1,64]{1,0:T(1,128)}, f32[1]{0:T(128)}) custom-call(s32[3]{0:T(128)} %pad_add_fusion.place_ref, f32[1088,128]{1,0:T(8,128)S(1)} %bitcast.13, f32[1088,128]{1,0:T(8,128)S(1)} %collective-permute-done.4.far_ref, f32[128,128]{1,0:T(8,128)S(1)} %coupling.1.coupling_ref, f32[1,32]{1,0:T(1,128)} %bitcast.16, f32[8,128]{1,0:T(8,128)S(1)} %get-tuple-element.13.extra_ref), custom_call_target="tpu_custom_call" | custom-call | tf_op jit(solution)/shard_map/gradient/pallas_call | solution.py:483
  (1 shorter events, 0.0 us)
Async XLA Ops:
  8.7 2.0 %collective-permute-start = (f32[4,264,128]{2,1,0:T(8,128)S(1)}, f32[4,264,128]{2,1,0:T(8,128)S(1)}, u32[]{:S(2)}, u32[]{:S(2)}) collective-permute-start(f32[4,264,128]{2,1,0:T(8,128)S(1)} %get-tuple-element.11), channel_id=1, source_target_pairs={{0,1},{1,0},{2,3},{3,2},{4,5},{5,4},{6,7},{7,6},{8,9},{9,8},{10,11... | collective-permute-start | bytes 1622024 | tf_op jit(solution)/shard_map/ppermute | solution.py:509
  10.8 10.8 %collective-permute-start.3 = (f32[264,128]{1,0:T(8,128)S(1)}, f32[264,128]{1,0:T(8,128)S(1)}, u32[]{:S(2)}, u32[]{:S(2)}) collective-permute-start(f32[264,128]{1,0:T(8,128)S(1)} %get-tuple-element.17), channel_id=1, source_target_pairs={{0,6},{1,7},{2,0},{3,1},{4,2},{5,3},{6,4},{7,5},{8,14},{9,15},{10,... | collective-permute-start | bytes 405512 | tf_op jit(solution)/shard_map/ppermute | solution.py:513
  15.0 6.5 %collective-permute-start.2 = (f32[264,128]{1,0:T(8,128)S(1)}, f32[264,128]{1,0:T(8,128)S(1)}, u32[]{:S(2)}, u32[]{:S(2)}) collective-permute-start(f32[264,128]{1,0:T(8,128)S(1)} %get-tuple-element.18), channel_id=1, source_target_pairs={{0,4},{1,5},{2,6},{3,7},{4,0},{5,1},{6,2},{7,3},{8,12},{9,13},{10,... | collective-permute-start | bytes 405512 | tf_op jit(solution)/shard_map/ppermute | solution.py:513
  16.1 8.9 %collective-permute-start.1 = (f32[264,128]{1,0:T(8,128)S(1)}, f32[264,128]{1,0:T(8,128)S(1)}, u32[]{:S(2)}, u32[]{:S(2)}) collective-permute-start(f32[264,128]{1,0:T(8,128)S(1)} %get-tuple-element.19), channel_id=1, source_target_pairs={{0,2},{1,3},{2,4},{3,5},{4,6},{5,7},{6,0},{7,1},{8,10},{9,11},{10,... | collective-permute-start | bytes 405512 | tf_op jit(solution)/shard_map/ppermute | solution.py:513
  58.2 4.2 %collective-permute-start.4 = (f32[1088,128]{1,0:T(8,128)S(1)}, f32[1088,128]{1,0:T(8,128)S(1)}, u32[]{:S(2)}, u32[]{:S(2)}) collective-permute-start(f32[1088,128]{1,0:T(8,128)S(1)} %bitcast.12), channel_id=1, source_target_pairs={{0,1},{1,0},{2,3},{3,2},{4,5},{5,4},{6,7},{7,6},{8,9},{9,8},{10,11... | collective-permute-start | bytes 1671176 | tf_op jit(solution)/shard_map/ppermute | solution.py:520

commit v3 on v2

--- a/solution.py
+++ b/solution.py
@@ -11,6 +11,7 @@
 COMMON = 64
 STEP_BLOCKS = 8
 ROWS_SENT = 264
+AHEAD = True
 WIDTH = 2176
 LINES = WIDTH // 128
 AXES = ("psr", "toa")
@@ -19,6 +20,11 @@
 f32 = jnp.float32
 
 
+def location():
+    toa = lax.axis_index("toa")
+    return toa >> 1, toa & 1, lax.axis_index("psr") * 4 + (toa >> 1)
+
+
 def in_vmem(value):
     return pltpu.with_memory_space_constraint(value, pltpu.VMEM)
 
@@ -32,55 +38,104 @@
 
 
 def lane_bcast(value, lane):
-    return jnp.broadcast_to(value[:, lane : lane + 1], value.shape)
+    index = jnp.full(value.shape, lane, jnp.int32)
+    return jnp.take_along_axis(value, index, axis=1, mode="promise_in_bounds")
 
 
 def total(value):
     return jnp.sum(jnp.sum(value, axis=0, keepdims=True), axis=1, keepdims=True)
 
 
-def eliminate_rows(tiles, first_lane, log_sum):
+def summed_tree(parts):
+    while len(parts) > 1:
+        joined = [u + v for u, v in zip(parts[::2], parts[1::2])]
+        parts = joined + ([parts[-1]] if len(parts) % 2 else [])
+    return parts[0]
+
+
+def invert_block(cols, log_sum):
+    row = iota((8, 128), 0)
+    for i in range(0, 8, 2):
+        first, second = row == i, row == i + 1
+        c0, c1 = cols[i], cols[i + 1]
+        p, q = sub_bcast(c0, i), sub_bcast(c1, i)
+        r, s = sub_bcast(c0, i + 1), sub_bcast(c1, i + 1)
+        det = p * s - q * r
+        inverse = 1.0 / det
+        log_sum = log_sum + jnp.log(det)
+        for k in range(8):
+            if k not in (i, i + 1):
+                u, v = sub_bcast(cols[k], i), sub_bcast(cols[k], i + 1)
+                n0 = s * u - q * v
+                n1 = p * v - r * u
+                moved = cols[k] - (c0 * n0 + c1 * n1) * inverse
+                moved = jnp.where(first, n0 * inverse, moved)
+                cols[k] = jnp.where(second, n1 * inverse, moved)
+        left = jnp.where(first, s, jnp.where(second, -r, c1 * r - c0 * s))
+        right = jnp.where(first, -q, jnp.where(second, p, c0 * q - c1 * p))
+        cols[i] = left * inverse
+        cols[i + 1] = right * inverse
+    return cols, log_sum
+
+
+class Board:
+    def __init__(self, ref):
+        self.ref, self.used = ref, 0
+
+    def rows(self, value):
+        at = self.used
+        self.used = at + 1
+        self.ref[at] = value
+        return [self.ref[at, k : k + 1, :] for k in range(8)]
+
+
+def eliminate_rows(tiles, first_lane, log_sum, board, whole, ahead=True):
     count = len(tiles)
     width = len(tiles[0])
-    row = iota((8, 128), 0)
+    before, after = [], []
+
+    def columns(a, b):
+        at = first_lane + 8 * b
+        return [lane_bcast(tiles[a][at // 128], at % 128 + k) for k in range(8)]
+
+    cols = columns(0, 0)
     for b in range(count):
-        at = first_lane + 8 * b
-        tile, lane = at // 128, at % 128
-        cols = [lane_bcast(tiles[b][tile], lane + k) for k in range(8)]
-        for i in range(8):
-            here = row == i
-            pivot = sub_bcast(cols[i], i)
-            inverse = 1.0 / pivot
-            log_sum = log_sum + jnp.log(pivot)
-            column = cols[i]
-            for k in range(8):
-                if k != i:
-                    scaled = sub_bcast(cols[k], i) * inverse
-                    cols[k] = jnp.where(here, scaled, cols[k] - column * scaled)
-            cols[i] = jnp.where(here, inverse, -column * inverse)
-        fresh = []
+        cols, log_sum = invert_block(cols, log_sum)
+        last = b + 1 == count
+        factors = {}
+        if not last and ahead:
+            factor = columns(b + 1, b)
+            factors[b + 1] = factor
+            coming = columns(b + 1, b + 1)
+            spots = [board.rows(value) for value in factor]
+            for j in range(8):
+                solved = summed_tree([cols[m] * spots[m][j] for m in range(8)])
+                change = summed_tree([factor[k] * sub_bcast(solved, k) for k in range(8)])
+                coming[j] = coming[j] - change
+        fresh, spread = [], []
         for t in range(width):
-            parts = [cols[k] * sub_bcast(tiles[b][t], k) for k in range(8)]
-            while len(parts) > 1:
-                parts = [u + v for u, v in zip(parts[::2], parts[1::2])]
-            fresh.append(parts[0])
-        spread = [[sub_bcast(fresh[t], k) for k in range(8)] for t in range(width)]
-        for a in range(count):
+            rows = board.rows(tiles[b][t])
+            fresh.append(summed_tree([cols[k] * rows[k] for k in range(8)]))
+            spread.append(board.rows(fresh[t]))
+        before.append(tiles[b])
+        after.append(fresh)
+        for a in range(0 if whole else b + 1, count):
             if a != b:
-                factor = [lane_bcast(tiles[a][tile], lane + k) for k in range(8)]
-                for t in range(width):
-                    value = tiles[a][t]
-                    for k in range(8):
-                        value = value - factor[k] * spread[t][k]
-                    tiles[a][t] = value
-        tiles[b] = fresh
-    return tiles, log_sum
+                factor = factors[a] if a in factors else columns(a, b)
+                tiles[a] = [
+                    tiles[a][t] - summed_tree([factor[k] * spread[t][k] for k in range(8)])
+                    for t in range(width)
+                ]
+        if whole:
+            tiles[b] = fresh
+        if not last:
+            cols = coming if ahead else columns(b + 1, b + 1)
+    return tiles, before, after, log_sum
 
 
 def gram_kernel(
     pulsar_ref,
     rows_ref,
-    place_ref,
     design_ref,
     weight_ref,
     resid_ref,
@@ -157,8 +212,7 @@
     row, col = iota((128, 128), 0), iota((128, 128), 1)
     line = iota((8, 128), 0)
     spot = iota((8, 128), 1)
-    height = place_ref[0]
-    core = place_ref[1]
+    height, core, _ = location()
 
     def pack(out_ref, s, k):
         @pl.when(counts[k] == 0)
@@ -191,7 +245,7 @@
         pack(mine_ref, s, base + core)
 
 
-def gram_parts(place, design, weight, residuals, slot_pulsar, slot_rows):
+def gram_parts(design, weight, residuals, slot_pulsar, slot_rows):
     slots = design.shape[0]
     piece = pltpu.VMEM((4, ROWS_SENT, 128), f32)
     smem = pl.BlockSpec(memory_space=pltpu.SMEM)
@@ -199,7 +253,7 @@
     hbm = pl.BlockSpec(memory_space=pl.ANY)
     return pl.pallas_call(
         gram_kernel,
-        in_specs=[smem, smem, smem, hbm, vmem, vmem],
+        in_specs=[smem, smem, hbm, vmem, vmem],
         out_specs=[vmem, vmem],
         scratch_shapes=[
             pltpu.VMEM((slots, 128, COLUMNS), jnp.bfloat16),
@@ -212,11 +266,11 @@
         ],
         out_shape=[piece, piece],
         name="gram",
-    )(slot_pulsar, slot_rows, place, design, weight, residuals)
-
-
-def coupling_kernel(place_ref, directions_ref, out_ref):
-    core = place_ref[1]
+    )(slot_pulsar, slot_rows, design, weight, residuals)
+
+
+def coupling_kernel(directions_ref, out_ref, board_ref):
+    _, core, _ = location()
     row, col = iota((128, 128), 0), iota((128, 128), 1)
     source = jnp.where(col < 64, 2 * col + core, 2 * col - 127 - core)
     chosen = (row == source).astype(f32)
@@ -235,22 +289,21 @@
     tiles = [
         [correlation[8 * a : 8 * a + 8, :], identity[8 * a : 8 * a + 8, :]] for a in range(16)
     ]
-    tiles, _ = eliminate_rows(tiles, 0, jnp.zeros((8, 128), f32))
+    board = Board(board_ref)
+    tiles, _, _, _ = eliminate_rows(tiles, 0, jnp.zeros((8, 128), f32), board, True, AHEAD)
     for a in range(16):
         out_ref[8 * a : 8 * a + 8, :] = tiles[a][1]
 
 
-def coupling_inverse(place, directions):
+def coupling_inverse(directions):
     return pl.pallas_call(
         coupling_kernel,
-        in_specs=[
-            pl.BlockSpec(memory_space=pltpu.SMEM),
-            pl.BlockSpec(memory_space=pltpu.VMEM),
-        ],
+        in_specs=[pl.BlockSpec(memory_space=pltpu.VMEM)],
         out_specs=pl.BlockSpec(memory_space=pltpu.VMEM),
         out_shape=pltpu.VMEM((128, 128), f32),
+        scratch_shapes=[pltpu.VMEM((16 * 12, 8, 128), f32)],
         name="coupling",
-    )(place, directions)
+    )(directions)
 
 
 def power_column(spectrum_ref):
@@ -261,7 +314,6 @@
 
 
 def own_kernel(
-    place_ref,
     kept,
     part0,
     part1,
@@ -273,7 +325,7 @@
     sent_ref,
     extra_ref,
     logdet_ref,
-    work,
+    board_ref,
 ):
     row, col = iota((128, 128), 0), iota((128, 128), 1)
 
@@ -291,49 +343,65 @@
     upper = jnp.where(col == row, rest[0:1, :] + prior[:, 0:128], upper)
     lower = jnp.where(col <= row, packed, turned)
     lower = jnp.where(col == row, lower + prior[:, 128:256], lower)
-    work[0:128, 0:128] = upper
-    work[128:256, 128:256] = lower
-    work[128:256, 0:128] = cross
-    work[0:128, 128:256] = cross.T
     side = rest.T
-    work[0:128, 256:384] = jnp.broadcast_to(side[:, 1:2], (128, 128))
-    work[128:256, 256:384] = jnp.broadcast_to(side[:, 2:3], (128, 128))
-
+    lane = iota((64, 128), 1)
     log_sum = jnp.zeros((8, 128), f32)
-    quadratic = jnp.zeros((64, 128), f32)
-    for panel in range(3):
-        at = COMMON + 64 * panel
-        old = work[at : at + 64, :]
-        tiles = [
-            [old[8 * a : 8 * a + 8, 128 * t : 128 * t + 128] for t in range(3)] for a in range(8)
+
+    board = Board(board_ref)
+
+    def panel_of(parts, at, log_sum):
+        tiles = [[part[8 * a : 8 * a + 8, :] for part in parts] for a in range(8)]
+        _, before, after, log_sum = eliminate_rows(tiles, at, log_sum, board, False)
+        old, new = [
+            [jnp.concatenate([rows[a][t] for a in range(8)], axis=0) for t in range(len(parts))]
+            for rows in (before, after)
         ]
-        tiles, log_sum = eliminate_rows(tiles, at, log_sum)
-        fresh = [jnp.concatenate([tiles[a][t] for a in range(8)], axis=0) for t in range(3)]
-        quadratic = quadratic + old[:, 256:384] * fresh[2]
-        final = panel == 2
-        for t in (0,) if final else (0, 1):
-            left = old[:, 128 * t : 128 * t + 128]
-            for u in (0, 2) if final else (0, 1, 2):
-                change = lax.dot_general(
-                    left,
-                    fresh[u],
-                    (((0,), (0,)), ((), ())),
-                    precision=highest,
-                    preferred_element_type=f32,
-                )
-                where = (slice(128 * t, 128 * t + 128), slice(128 * u, 128 * u + 128))
-                work[where] = work[where] - change
-
-    own = place_ref[2]
+        return old, new, log_sum
+
+    def product(left, right):
+        return lax.dot_general(
+            left,
+            right,
+            (((0,), (0,)), ((), ())),
+            precision=highest,
+            preferred_element_type=f32,
+        )
+
+    turned_cross = cross.T
+    right_top = jnp.broadcast_to(side[:, 1:2], (128, 128))
+    right_low = jnp.broadcast_to(side[:, 2:3], (128, 128))
+    final = jnp.where(lane < 64, upper[0:64, :], right_top[0:64, :])
+    low = [jnp.where(iota((128, 128), 1) < 64, cross, right_low), lower]
+
+    parts = [upper[64:128, :], turned_cross[64:128, :], right_top[64:128, :]]
+    old, fresh, log_sum = panel_of(parts, 64, log_sum)
+    quadratic = old[2] * fresh[2]
+    first = jnp.where(lane < 64, fresh[0], fresh[2])
+    change = product(old[1], jnp.concatenate([first, fresh[1]], axis=1))
+    low = [low[0] - change[:, 0:128], low[1] - change[:, 128:256]]
+    final = final - product(old[0][:, 0:64], first)
+
+    parts = [low[0][0:64, :], low[1][0:64, :]]
+    old, fresh, log_sum = panel_of(parts, 128, log_sum)
+    quadratic = quadratic + old[0] * fresh[0]
+    change = product(old[1][:, 64:128], jnp.concatenate(fresh, axis=1))
+    final = final - product(old[0][:, 0:64], fresh[0])
+
+    parts = [low[0][64:128, :] - change[:, 0:128], low[1][64:128, :] - change[:, 128:256]]
+    old, fresh, log_sum = panel_of(parts, 192, log_sum)
+    quadratic = quadratic + old[0] * fresh[0]
+    final = final - product(old[0][:, 0:64], fresh[0])
+
+    _, _, own = location()
     mine = jnp.where((row == own) & (col == own), coupling_ref[...], 0.0)
     self_coupling = total(mine)
     power = power_column(spectrum_ref)
     row64, col64 = iota((64, 128), 0), iota((64, 128), 1)
-    block = work[0:64, 0:128]
+    block = final
     block = jnp.where(row64 == col64, block + self_coupling * power, block)
     block = jnp.where(col64 < 64, block, jnp.where(col64 == row64 + 64, 1.0, 0.0))
     tiles = [[block[8 * a : 8 * a + 8, :]] for a in range(8)]
-    tiles, log_sum = eliminate_rows(tiles, 0, log_sum)
+    tiles, _, _, log_sum = eliminate_rows(tiles, 0, log_sum, board, True)
     solved = jnp.concatenate([tiles[a][0] for a in range(8)], axis=0)
     inverse = pltpu.roll(solved, 64, 1)
     top, bottom = inverse[0:32, :], inverse[32:64, :]
@@ -345,39 +413,38 @@
         iota((16, 128), 1) < 64, folded[0:16, :], pltpu.roll(folded[16:32, :], 64, 1)
     )
     diagonal = jnp.sum(jnp.where(row32 == col32, top, 0.0), axis=0, keepdims=True)
-    target = work[0:64, 256:384]
-    target_line = jnp.concatenate([target, target], axis=0).T[0:1, :]
+    target = final
+    target_line = jnp.concatenate([target, target], axis=0).T[64:65, :]
     final_line = jnp.where(iota((1, 128), 1) < 64, diagonal, target_line)
     whole = jnp.concatenate([lines, final_line], axis=0)
     whole = jnp.concatenate([whole] * 8, axis=0)
     for i in range(8):
         sent_ref[8 * LINES * i : 8 * LINES * (i + 1), :] = whole
     spent = jnp.sum(quadratic, axis=0, keepdims=True)
-    left_over = rest[3:4, 0:1] - spent[:, 0:1]
+    left_over = rest[3:4, 0:1] - spent[:, 64:65]
     line = iota((8, 128), 0)
     extra_ref[...] = jnp.where(line == 0, left_over, rest[3:4, 1:2])
     logdet_ref[0] = log_sum[0, 0] / COLUMNS
 
 
-def own_terms(place, parts, own_prior, spectrum, coupling):
+def own_terms(parts, own_prior, spectrum, coupling):
     vmem = pl.BlockSpec(memory_space=pltpu.VMEM)
     smem = pl.BlockSpec(memory_space=pltpu.SMEM)
     return pl.pallas_call(
         own_kernel,
-        in_specs=[smem] + [vmem] * 8,
+        in_specs=[vmem] * 8,
         out_specs=[vmem, vmem, smem],
         out_shape=[
             pltpu.VMEM((64 * LINES, 128), f32),
             pltpu.VMEM((8, 128), f32),
             jax.ShapeDtypeStruct((1,), f32),
         ],
-        scratch_shapes=[pltpu.VMEM((COLUMNS, 384), f32)],
+        scratch_shapes=[pltpu.VMEM((32 * 14, 8, 128), f32)],
         name="own",
-    )(place, *map(in_vmem, parts), own_prior, spectrum, in_vmem(coupling))
+    )(*map(in_vmem, parts), own_prior, spectrum, in_vmem(coupling))
 
 
 def gradient_kernel(
-    place_ref,
     near_ref,
     far_ref,
     coupling_ref,
@@ -387,6 +454,7 @@
     chi_ref,
     flat,
     inverse,
+    target,
     resid,
     direction,
     mapped,
@@ -394,49 +462,43 @@
     turned,
 ):
     for i in range(LINES):
-        where = slice(128 * i, 128 * i + 128)
         rows = pl.ds(i, 64, stride=LINES)
-        flat[where, :] = jnp.concatenate([near_ref[rows, :], far_ref[rows, :]], axis=0).T
+        both = jnp.concatenate([near_ref[rows, :], far_ref[rows, :]], axis=0).T
+        for m in range(0, 128, 8):
+            flat[pl.ds(m * LINES + i, 8, stride=LINES), :] = both[m : m + 8, :]
     line = iota((8, 128), 0)
 
-    def start(r):
-        return (r % 16) * 128 + (r // 16) * 64
-
-    def across(c, offset):
-        return flat[pl.ds(start(c) + offset, 8, stride=128), :]
+    def straight_of(r, c):
+        return flat[pl.ds((64 * (r // 16) + c) * LINES + r % 16, 8, stride=LINES), :]
+
+    def crossed_of(c, r):
+        at = (64 * (c // 16) + r) * LINES + c % 16
+        return flat[at : at + 8, :]
 
     for r in range(32):
-        at = start(r)
-        corner = flat[2048 + r : 2049 + r, :]
+        corner = flat[r * LINES + 16 : r * LINES + 17, :]
         for c in range(0, 32, 8):
-            straight = None if c + 7 < r else flat[at + c : at + c + 8, :]
-            crossed = None if c > r else across(c, r)
-            if straight is None:
-                first = second = crossed
-                second = None
-            if crossed is None:
-                first = straight
-            if straight is not None and crossed is not None:
+            if c > r:
+                upper, lower = straight_of(r, c), crossed_of(c, r)
+            elif c + 7 < r:
+                upper, lower = crossed_of(c, r), straight_of(r, c)
+            else:
                 index = line + c
-                first = jnp.where(index > r, straight, crossed)
-                first = jnp.where(index == r, corner, first)
-            inverse[r, c : c + 8, :] = first
-            low = None if c > r else flat[at + c : at + c + 8, :]
-            high = None if c + 7 <= r else across(c, r)
-            if low is None:
-                value = high
-            elif high is None:
-                value = low
-            else:
-                value = jnp.where(line + c <= r, low, high)
-            inverse[32 + r, 32 + c : 40 + c, :] = value
-            inverse[r, 32 + c : 40 + c, :] = flat[at + 32 + c : at + 40 + c, :]
-            inverse[32 + r, c : c + 8, :] = across(c, 32 + r)
+                straight, crossed = straight_of(r, c), crossed_of(c, r)
+                upper = jnp.where(index > r, straight, crossed)
+                upper = jnp.where(index == r, corner, upper)
+                lower = jnp.where(index <= r, straight, crossed)
+            inverse[r, c : c + 8, :] = upper
+            inverse[32 + r, 32 + c : 40 + c, :] = lower
+            inverse[r, 32 + c : 40 + c, :] = straight_of(r, 32 + c)
+            inverse[32 + r, c : c + 8, :] = crossed_of(c, 32 + r)
+    for c in range(0, 64, 8):
+        target[c : c + 8, :] = flat[pl.ds((64 + c) * LINES + 16, 8, stride=LINES), :]
 
     row, col = iota((128, 128), 0), iota((128, 128), 1)
     mixing = jnp.where(row == col, 0.0, coupling_ref[...])
     power = power_column(spectrum_ref)
-    resid[...] = flat[2112:2176, :]
+    resid[...] = target[...]
     direction[...] = jnp.zeros((64, 128), f32)
     mapped[...] = jnp.zeros((64, 128), f32)
     answer[...] = jnp.zeros((64, 128), f32)
@@ -465,9 +527,9 @@
         return inner_next, curved
 
     lax.fori_loop(0, ITERS, iterate, (jnp.ones((1, 1), f32), jnp.zeros((1, 1), f32)))
-    own = place_ref[2]
+    _, _, own = location()
     value = answer[...]
-    gained = jnp.sum(flat[2112:2176, :] * value, axis=0, keepdims=True)
+    gained = jnp.sum(target[...] * value, axis=0, keepdims=True)
     lane = iota((1, 128), 1)
     gained = jnp.sum(jnp.where(lane == own, gained, 0.0), axis=1, keepdims=True)
     chi = (extra_ref[0:1, 0:1] - gained) / extra_ref[1:2, 0:1]
@@ -476,13 +538,13 @@
     coeffs_ref[...] = turned[pl.ds(own, 1), :][:, 0:64]
 
 
-def conjugate(place, near, far, coupling, spectrum, extra):
+def conjugate(near, far, coupling, spectrum, extra):
     vmem = pl.BlockSpec(memory_space=pltpu.VMEM)
     smem = pl.BlockSpec(memory_space=pltpu.SMEM)
     square = pltpu.VMEM((64, 128), f32)
     return pl.pallas_call(
         gradient_kernel,
-        in_specs=[smem] + [vmem] * 5,
+        in_specs=[vmem] * 5,
         out_specs=[vmem, smem],
         out_shape=[jax.ShapeDtypeStruct((1, COMMON), f32), jax.ShapeDtypeStruct((1,), f32)],
         scratch_shapes=[
@@ -492,33 +554,30 @@
             square,
             square,
             square,
+            square,
             pltpu.VMEM((128, 128), f32),
         ],
         name="gradient",
-    )(place, in_vmem(near), in_vmem(far), in_vmem(coupling), spectrum, in_vmem(extra))
+    )(in_vmem(near), in_vmem(far), in_vmem(coupling), spectrum, in_vmem(extra))
 
 
 def body(design, noise_weight, residuals, slot_pulsar, slot_rows, own_prior, spectrum, directions):
-    toa = lax.axis_index("toa")
-    device = lax.axis_index("psr") * lax.axis_size("toa") + toa
     count = lax.axis_size("psr") * lax.axis_size("toa")
-    core = toa % 2
-    place = jnp.stack([toa // 2, core, device // 2]).astype(jnp.int32)
     spectrum = spectrum.reshape(1, -1)
-    mine, other = gram_parts(place, design, noise_weight, residuals, slot_pulsar, slot_rows)
+    mine, other = gram_parts(design, noise_weight, residuals, slot_pulsar, slot_rows)
     got = lax.ppermute(other, "toa", [(u, u ^ 1) for u in range(8)])
     parts = [mine, got]
     for s in range(1, 4):
         part = mine[s] + got[s]
         parts.append(lax.ppermute(part, "toa", [(u, (u + 2 * s) % 8) for u in range(8)]))
-    coupling = coupling_inverse(place, directions)
-    sent, extra, log_dets = own_terms(place, parts, own_prior, spectrum, coupling)
+    coupling = coupling_inverse(directions)
+    sent, extra, log_dets = own_terms(parts, own_prior, spectrum, coupling)
     groups = [list(range(c, count, 2)) for c in range(2)]
     sent = sent.reshape(64, 1, WIDTH)
     near = lax.all_to_all(sent, AXES, 0, 0, tiled=True, axis_index_groups=groups)
     near = near.reshape(64 * LINES, 128)
     far = lax.ppermute(near, "toa", [(u, u ^ 1) for u in range(8)])
-    coeffs, chi_square = conjugate(place, near, far, coupling, spectrum, extra)
+    coeffs, chi_square = conjugate(near, far, coupling, spectrum, extra)
     return (coeffs, log_dets, chi_square)
 
 

time: 69.2 us -> 62.9 us (0.909)
  Pallas kernels: 31.3 us -> 22.5 us
  starting transfers between devices: 8.39 us -> 13.3 us
  blocking collectives: 20.8 us -> 19.3 us
    pallas_call x3, Pallas kernels: 26.2 us -> 17.2 us  [the longest x1 7.48 us: own_terms(): pl.pallas_call(own_kernel, in_specs=[vmem] * 8, out_specs=[vmem, vmem, sm...]
    ppermute x1, starting transfers between devices: 0.09 us -> 4.76 us  [body(): got = lax.ppermute(other, 'toa', [(u, u ^ 1) for u in range(8)])]
    all_to_all x1, blocking collectives: 20.8 us -> 19.3 us  [body(): lax.all_to_all(sent, AXES, 0, 0, tiled=True, axis_index_groups=groups)]
  transfers between devices with their start and end apart: 5 -> 5, of which waited for: 3 -> 4; matrix products, arithmetic and copies ran while one was open for 0% -> 0% of each run, Pallas kernels for 7% -> 8%
where the time goes in v3:
time: 62.9 us; the launch traced here: 62.5 us
  Pallas kernels  22.5 us (36%)
  blocking collectives  19.3 us (31%)
  starting transfers between devices  13.3 us (21%)
  waiting for transfers between devices  6.49 us (10%)
  between operations  0.83 us (1%)
    all_to_all x1, blocking collectives, body(): lax.all_to_all(sent, AXES, 0, 0, tiled=True, axis_index_groups=groups)  19.3 us
    pallas_call x1, Pallas kernels, own_terms(): pl.pallas_call(own_kernel, in_specs=[vmem] * 8, out_specs=[vmem, vmem, sm...  7.48 us
    ppermute x3, starting transfers between devices, body(): lax.ppermute(part, 'toa', [(u, (u + 2 * s) % 8) for u in range(8)])  5.89 us
    pallas_call x1, Pallas kernels, conjugate(): pl.pallas_call(gradient_kernel, in_specs=[vmem] * 5, out_specs=[vmem, sme...  5.84 us
    pallas_call x1, Pallas kernels, coupling_inverse(): pl.pallas_call(coupling_kernel, in_specs=[pl.BlockSpec(memory_space=pltpu...  5.3 us
    ppermute x1, starting transfers between devices, body(): got = lax.ppermute(other, 'toa', [(u, u ^ 1) for u in range(8)])  4.76 us
    pallas_call x1, Pallas kernels, gram_parts(): pl.pallas_call(gram_kernel, in_specs=[smem, smem, hbm, vmem, vmem], out_s...  3.88 us
    ppermute x3, waiting for transfers between devices, body(): lax.ppermute(part, 'toa', [(u, (u + 2 * s) % 8) for u in range(8)])  3.35 us
  transfers between devices with their start and end apart: 5, of which 4 were waited for; matrix products, arithmetic and copies ran while one was open for 0% of the time, Pallas kernels for 8%

profile of v3, /device:TPU:1, one launch (start us, length us, event | category | flops | bytes accessed | tf_op | source)
XLA Modules:
  0.0 62.5 jit_solution(18033050446827045297)
XLA Ops:
  0.6 3.9 %gram.1 = (f32[4,264,128]{2,1,0:T(8,128)S(1)}, f32[4,264,128]{2,1,0:T(8,128)S(1)}) custom-call(s32[96]{0:T(128)} %pulsar_ref.1, s32[96]{0:T(128)} %rows_ref.1, bf16[96,128,256]{2,1,0:T(8,128)(2,1)} %design_ref.1, f32[96,128]{1,0:T(8,128)} %weight_ref.1, bf16[96,128]{1,0:T(8,128)(2,1)} %resid_ref.1), custom_call_target="tpu_custom_call" | custom-call | tf_op jit(solution)/shard_map/gram/pallas_call | solution.py:254
  4.5 4.8 %collective-permute-start = (f32[4,264,128]{2,1,0:T(8,128)S(1)}, f32[4,264,128]{2,1,0:T(8,128)S(1)}, u32[]{:S(2)}, u32[]{:S(2)}) collective-permute-start(f32[4,264,128]{2,1,0:T(8,128)S(1)} %get-tuple-element.11), channel_id=1, source_target_pairs={{0,1},{1,0},{2,3},{3,2},{4,5},{5,4},{6,7},{7,6},{8,9},{9,8},{10,11... | collective-permute-start | bytes 1622024 | tf_op jit(solution)/shard_map/ppermute | solution.py:568
  9.3 1.6 %collective-permute-done.part0 = f32[4,264,128]{2,1,0:T(8,128)S(1)} collective-permute-done((f32[4,264,128]{2,1,0:T(8,128)S(1)}, f32[4,264,128]{2,1,0:T(8,128)S(1)}, u32[]{:S(2)}, u32[]{:S(2)}) %collective-permute-start) | collective-permute-done | bytes 540704 | tf_op jit(solution)/shard_map/ppermute | solution.py:568
  10.9 5.2 %collective-permute-start.3 = (f32[264,128]{1,0:T(8,128)S(1)}, f32[264,128]{1,0:T(8,128)S(1)}, u32[]{:S(2)}, u32[]{:S(2)}) collective-permute-start(f32[264,128]{1,0:T(8,128)S(1)} %get-tuple-element.17), channel_id=1, source_target_pairs={{0,6},{1,7},{2,0},{3,1},{4,2},{5,3},{6,4},{7,5},{8,14},{9,15},{10,... | collective-permute-start | bytes 405512 | tf_op jit(solution)/shard_map/ppermute | solution.py:572
  16.1 0.0 collective-permute-start.2
  16.1 0.7 %collective-permute-start.1 = (f32[264,128]{1,0:T(8,128)S(1)}, f32[264,128]{1,0:T(8,128)S(1)}, u32[]{:S(2)}, u32[]{:S(2)}) collective-permute-start(f32[264,128]{1,0:T(8,128)S(1)} %get-tuple-element.19), channel_id=1, source_target_pairs={{0,2},{1,3},{2,4},{3,5},{4,6},{5,7},{6,0},{7,1},{8,10},{9,11},{10,... | collective-permute-start | bytes 405512 | tf_op jit(solution)/shard_map/ppermute | solution.py:572
  16.8 5.3 %coupling.1.coupling_ref = f32[128,128]{1,0:T(8,128)S(1)} custom-call(f32[3,128]{1,0:T(4,128)} %directions_ref.1), custom_call_target="tpu_custom_call" | custom-call | tf_op jit(solution)/shard_map/coupling/pallas_call | solution.py:299
  22.1 0.0 collective-permute-done.3.part3
  22.1 0.1 collective-permute-done.2.part2
  22.2 3.2 %collective-permute-done.1.part1 = f32[264,128]{1,0:T(8,128)S(1)} collective-permute-done((f32[264,128]{1,0:T(8,128)S(1)}, f32[264,128]{1,0:T(8,128)S(1)}, u32[]{:S(2)}, u32[]{:S(2)}) %collective-permute-start.1) | collective-permute-done | bytes 135200 | tf_op jit(solution)/shard_map/ppermute | solution.py:572
  25.4 7.5 %own.1 = (f32[1088,128]{1,0:T(8,128)S(1)}, f32[8,128]{1,0:T(8,128)S(1)}, f32[1]{0:T(128)}) custom-call(f32[4,264,128]{2,1,0:T(8,128)S(1)} %get-tuple-element.10.kept, f32[4,264,128]{2,1,0:T(8,128)S(1)} %collective-permute-done.part0, f32[264,128]{1,0:T(8,128)S(1)} %collective-permute-done.1.part1, f32[264,128]{1,0:T(8,128)S(1)} %collective-permute-done.2.part2, ...), custom_call_target="tpu_custom_call" | custom-call | tf_op jit(solution)/shard_map/own/pallas_call | solution.py:433
  32.9 19.3 %all_to_all.5 = f32[64,1,2176]{2,1,0:T(1,128)S(1)} all-to-all(f32[64,1,2176]{2,1,0:T(1,128)S(1)} %bitcast.11), channel_id=1, replica_groups={{0,2,4,6,8,10,12,14,16,18,20,22,24,26,28,30,32,34,36,38,40,42,44,46,48,..., dimensions={0} | all-to-all | bytes 1114112 | tf_op jit(solution)/shard_map/all_to_all | solution.py:577
  52.2 2.7 %collective-permute-start.4 = (f32[1088,128]{1,0:T(8,128)S(1)}, f32[1088,128]{1,0:T(8,128)S(1)}, u32[]{:S(2)}, u32[]{:S(2)}) collective-permute-start(f32[1088,128]{1,0:T(8,128)S(1)} %bitcast.9), channel_id=1, source_target_pairs={{0,1},{1,0},{2,3},{3,2},{4,5},{5,4},{6,7},{7,6},{8,9},{9,8},{10,11... | collective-permute-start | bytes 1671176 | tf_op jit(solution)/shard_map/ppermute | solution.py:579
  54.9 1.6 %collective-permute-done.4.far_ref = f32[1088,128]{1,0:T(8,128)S(1)} collective-permute-done((f32[1088,128]{1,0:T(8,128)S(1)}, f32[1088,128]{1,0:T(8,128)S(1)}, u32[]{:S(2)}, u32[]{:S(2)}) %collective-permute-start.4) | collective-permute-done | bytes 557088 | tf_op jit(solution)/shard_map/ppermute | solution.py:579
  56.5 5.8 %gradient.1 = (f32[1,64]{1,0:T(1,128)}, f32[1]{0:T(128)}) custom-call(f32[1088,128]{1,0:T(8,128)S(1)} %bitcast.10, f32[1088,128]{1,0:T(8,128)S(1)} %collective-permute-done.4.far_ref, f32[128,128]{1,0:T(8,128)S(1)} %coupling.1.coupling_ref, f32[1,32]{1,0:T(1,128)} %bitcast.13, f32[8,128]{1,0:T(8,128)S(1)} %get-tuple-element.13.extra_ref), custom_call_target="tpu_custom_call" | custom-call | tf_op jit(solution)/shard_map/gradient/pallas_call | solution.py:545
  (1 shorter events, 0.0 us)
Async XLA Ops:
  4.5 6.3 %collective-permute-start = (f32[4,264,128]{2,1,0:T(8,128)S(1)}, f32[4,264,128]{2,1,0:T(8,128)S(1)}, u32[]{:S(2)}, u32[]{:S(2)}) collective-permute-start(f32[4,264,128]{2,1,0:T(8,128)S(1)} %get-tuple-element.11), channel_id=1, source_target_pairs={{0,1},{1,0},{2,3},{3,2},{4,5},{5,4},{6,7},{7,6},{8,9},{9,8},{10,11... | collective-permute-start | bytes 1622024 | tf_op jit(solution)/shard_map/ppermute | solution.py:568
  10.9 11.2 %collective-permute-start.3 = (f32[264,128]{1,0:T(8,128)S(1)}, f32[264,128]{1,0:T(8,128)S(1)}, u32[]{:S(2)}, u32[]{:S(2)}) collective-permute-start(f32[264,128]{1,0:T(8,128)S(1)} %get-tuple-element.17), channel_id=1, source_target_pairs={{0,6},{1,7},{2,0},{3,1},{4,2},{5,3},{6,4},{7,5},{8,14},{9,15},{10,... | collective-permute-start | bytes 405512 | tf_op jit(solution)/shard_map/ppermute | solution.py:572
  16.1 6.1 %collective-permute-start.2 = (f32[264,128]{1,0:T(8,128)S(1)}, f32[264,128]{1,0:T(8,128)S(1)}, u32[]{:S(2)}, u32[]{:S(2)}) collective-permute-start(f32[264,128]{1,0:T(8,128)S(1)} %get-tuple-element.18), channel_id=1, source_target_pairs={{0,4},{1,5},{2,6},{3,7},{4,0},{5,1},{6,2},{7,3},{8,12},{9,13},{10,... | collective-permute-start | bytes 405512 | tf_op jit(solution)/shard_map/ppermute | solution.py:572
  16.1 9.3 %collective-permute-start.1 = (f32[264,128]{1,0:T(8,128)S(1)}, f32[264,128]{1,0:T(8,128)S(1)}, u32[]{:S(2)}, u32[]{:S(2)}) collective-permute-start(f32[264,128]{1,0:T(8,128)S(1)} %get-tuple-element.19), channel_id=1, source_target_pairs={{0,2},{1,3},{2,4},{3,5},{4,6},{5,7},{6,0},{7,1},{8,10},{9,11},{10,... | collective-permute-start | bytes 405512 | tf_op jit(solution)/shard_map/ppermute | solution.py:572
  52.2 4.3 %collective-permute-start.4 = (f32[1088,128]{1,0:T(8,128)S(1)}, f32[1088,128]{1,0:T(8,128)S(1)}, u32[]{:S(2)}, u32[]{:S(2)}) collective-permute-start(f32[1088,128]{1,0:T(8,128)S(1)} %bitcast.9), channel_id=1, source_target_pairs={{0,1},{1,0},{2,3},{3,2},{4,5},{5,4},{6,7},{7,6},{8,9},{9,8},{10,11... | collective-permute-start | bytes 1671176 | tf_op jit(solution)/shard_map/ppermute | solution.py:579

commit v4 on v3

--- a/solution.py
+++ b/solution.py
@@ -10,6 +10,7 @@
 COLUMNS = 256
 COMMON = 64
 STEP_BLOCKS = 8
+IN_FLIGHT = 4
 ROWS_SENT = 264
 AHEAD = True
 WIDTH = 2176
@@ -139,14 +140,14 @@
     design_ref,
     weight_ref,
     resid_ref,
-    mine_ref,
     other_ref,
-    blocks,
     gram,
     fit,
     energy,
+    counts,
+    blocks,
+    turned,
     wide_resid,
-    counts,
     arrived,
 ):
     slots = weight_ref.shape[0]
@@ -156,7 +157,12 @@
         where = pl.ds(step * STEP_BLOCKS, STEP_BLOCKS)
         return pltpu.make_async_copy(design_ref.at[where], blocks.at[where], arrived.at[step])
 
-    for step in range(steps):
+    def turn(step):
+        load(step).wait()
+        for i in range(STEP_BLOCKS):
+            turned[step & 1, :, 128 * i : 128 * i + 128] = blocks[step * STEP_BLOCKS + i].T
+
+    for step in range(IN_FLIGHT):
         load(step).start()
     gram[...] = jnp.zeros(gram.shape, f32)
     fit[...] = jnp.zeros(fit.shape, f32)
@@ -165,9 +171,9 @@
         counts[k] = 0
     wide_resid[...] = resid_ref[...].astype(f32)
     lane = iota((1, 128), 1)
+    turn(0)
 
     def one_step(step, carry):
-        load(step).wait()
         at = step * STEP_BLOCKS
         pulsars = [pulsar_ref[at + i] for i in range(STEP_BLOCKS)]
         rows = [rows_ref[at + i] for i in range(STEP_BLOCKS)]
@@ -176,12 +182,24 @@
             same = same & (pulsars[i] == pulsars[0])
         low = jnp.where(same, pulsars[0], 0)
         high = jnp.where(same, pulsars[0] + 1, GROUP_PULSARS)
+        following = jnp.minimum(step + 1, steps - 1)
+
+        @pl.when(step + IN_FLIGHT < steps)
+        def _():
+            load(step + IN_FLIGHT).start()
+
+        @pl.when(step + 1 < steps)
+        def _():
+            load(following).wait()
+
+        def turn_next():
+            for i in range(STEP_BLOCKS):
+                block = blocks[following * STEP_BLOCKS + i]
+                turned[(step + 1) & 1, :, 128 * i : 128 * i + 128] = block.T
 
         def one_pulsar(pulsar, carry):
             valid = [jnp.where(pulsars[i] == pulsar, rows[i], 0) for i in range(STEP_BLOCKS)]
-            number = valid[0]
-            for i in range(1, STEP_BLOCKS):
-                number = number + valid[i]
+            number = sum(valid[1:], valid[0])
 
             @pl.when(number > 0)
             def _():
@@ -189,8 +207,8 @@
                 for i in range(STEP_BLOCKS):
                     weight = jnp.where(lane < valid[i], weight_ref[pl.ds(at + i, 1), :], 0.0)
                     resid = wide_resid[pl.ds(at + i, 1), :]
-                    turned = blocks[at + i].T.astype(f32)
-                    weighted = (turned * weight).astype(jnp.bfloat16)
+                    block = turned[step & 1, :, 128 * i : 128 * i + 128].astype(f32)
+                    weighted = (block * weight).astype(jnp.bfloat16)
                     pieces.append(weighted)
                     product = weighted.astype(f32) * resid
                     square = weight * resid * resid
@@ -202,47 +220,58 @@
                 fit[pulsar] = fit[pulsar] + fitted
                 energy[pl.ds(pulsar, 1), :] = energy[pl.ds(pulsar, 1), :] + squares
                 counts[pulsar] = counts[pulsar] + number
+                turn_next()
 
             return carry
 
-        return lax.fori_loop(low, high, one_pulsar, carry)
+        lax.fori_loop(low, high, one_pulsar, carry)
+
+        @pl.when(sum(rows[1:], rows[0]) == 0)
+        def _():
+            turn_next()
+
+        return carry
 
     lax.fori_loop(0, steps, one_step, 0)
-
+    height, core, _ = location()
+    for s in range(4):
+        pack(other_ref, s, 2 * ((height + s) & 3) + 1 - core, gram, fit, energy, counts)
+
+
+def pack(out_ref, s, k, gram, fit, energy, counts):
     row, col = iota((128, 128), 0), iota((128, 128), 1)
     line = iota((8, 128), 0)
     spot = iota((8, 128), 1)
+
+    @pl.when(counts[k] == 0)
+    def _():
+        out_ref[s] = jnp.zeros((ROWS_SENT, 128), f32)
+
+    @pl.when(counts[k] > 0)
+    def _():
+        upper = gram[k, 0:128, 0:128]
+        lower = gram[k, 128:256, 128:256]
+        upper = 0.5 * (upper + upper.T)
+        lower = 0.5 * (lower + lower.T)
+        cross = 0.5 * (gram[k, 128:256, 0:128] + gram[k, 0:128, 128:256].T)
+        out_ref[s, 0:128, :] = jnp.where(col > row, upper, lower)
+        out_ref[s, 128:256, :] = cross
+        diagonal = jnp.sum(jnp.where(col == row, upper, 0.0), axis=0, keepdims=True)
+        first = jnp.sum(fit[k, 0:128, :].T, axis=0, keepdims=True)
+        second = jnp.sum(fit[k, 128:256, :].T, axis=0, keepdims=True)
+        power = jnp.sum(energy[pl.ds(k, 1), :], axis=1, keepdims=True)
+        number = counts[k].astype(f32)
+        last = jnp.where(spot == 0, power, jnp.where(spot == 1, number, 0.0))
+        rest = jnp.where(line == 3, last, 0.0)
+        rest = jnp.where(line == 0, diagonal, rest)
+        rest = jnp.where(line == 1, first, rest)
+        out_ref[s, 256:264, :] = jnp.where(line == 2, second, rest)
+
+
+def keep_kernel(counts, gram, fit, energy, mine_ref):
     height, core, _ = location()
-
-    def pack(out_ref, s, k):
-        @pl.when(counts[k] == 0)
-        def _():
-            out_ref[s] = jnp.zeros((ROWS_SENT, 128), f32)
-
-        @pl.when(counts[k] > 0)
-        def _():
-            upper = gram[k, 0:128, 0:128]
-            lower = gram[k, 128:256, 128:256]
-            upper = 0.5 * (upper + upper.T)
-            lower = 0.5 * (lower + lower.T)
-            cross = 0.5 * (gram[k, 128:256, 0:128] + gram[k, 0:128, 128:256].T)
-            out_ref[s, 0:128, :] = jnp.where(col > row, upper, lower)
-            out_ref[s, 128:256, :] = cross
-            diagonal = jnp.sum(jnp.where(col == row, upper, 0.0), axis=0, keepdims=True)
-            first = jnp.sum(fit[k, 0:128, :].T, axis=0, keepdims=True)
-            second = jnp.sum(fit[k, 128:256, :].T, axis=0, keepdims=True)
-            power = jnp.sum(energy[pl.ds(k, 1), :], axis=1, keepdims=True)
-            number = counts[k].astype(f32)
-            last = jnp.where(spot == 0, power, jnp.where(spot == 1, number, 0.0))
-            rest = jnp.where(line == 3, last, 0.0)
-            rest = jnp.where(line == 0, diagonal, rest)
-            rest = jnp.where(line == 1, first, rest)
-            out_ref[s, 256:264, :] = jnp.where(line == 2, second, rest)
-
     for s in range(4):
-        base = 2 * ((height + s) & 3)
-        pack(other_ref, s, base + 1 - core)
-        pack(mine_ref, s, base + core)
+        pack(mine_ref, s, 2 * ((height + s) & 3) + core, gram, fit, energy, counts)
 
 
 def gram_parts(design, weight, residuals, slot_pulsar, slot_rows):
@@ -250,23 +279,35 @@
     piece = pltpu.VMEM((4, ROWS_SENT, 128), f32)
     smem = pl.BlockSpec(memory_space=pltpu.SMEM)
     vmem = pl.BlockSpec(memory_space=pltpu.VMEM)
-    hbm = pl.BlockSpec(memory_space=pl.ANY)
-    return pl.pallas_call(
+    other, gram, fit, energy, counts = pl.pallas_call(
         gram_kernel,
-        in_specs=[smem, smem, hbm, vmem, vmem],
-        out_specs=[vmem, vmem],
+        in_specs=[smem, smem, pl.BlockSpec(memory_space=pl.ANY), vmem, vmem],
+        out_specs=[vmem, vmem, vmem, vmem, smem],
         scratch_shapes=[
             pltpu.VMEM((slots, 128, COLUMNS), jnp.bfloat16),
+            pltpu.VMEM((2, COLUMNS, STEP_BLOCKS * 128), jnp.bfloat16),
+            pltpu.VMEM((slots, 128), f32),
+            pltpu.SemaphoreType.DMA((slots // STEP_BLOCKS,)),
+        ],
+        out_shape=[
+            piece,
             pltpu.VMEM((GROUP_PULSARS, COLUMNS, COLUMNS), f32),
             pltpu.VMEM((GROUP_PULSARS, COLUMNS, 128), f32),
             pltpu.VMEM((GROUP_PULSARS, 128), f32),
-            pltpu.VMEM((slots, 128), f32),
-            pltpu.SMEM((GROUP_PULSARS,), jnp.int32),
-            pltpu.SemaphoreType.DMA((slots // STEP_BLOCKS,)),
+            jax.ShapeDtypeStruct((GROUP_PULSARS,), jnp.int32),
         ],
-        out_shape=[piece, piece],
+        compiler_params=pltpu.CompilerParams(vmem_limit_bytes=24 << 20),
         name="gram",
     )(slot_pulsar, slot_rows, design, weight, residuals)
+    mine = pl.pallas_call(
+        keep_kernel,
+        in_specs=[smem, vmem, vmem, vmem],
+        out_specs=vmem,
+        out_shape=piece,
+        compiler_params=pltpu.CompilerParams(vmem_limit_bytes=24 << 20),
+        name="keep",
+    )(counts, in_vmem(gram), in_vmem(fit), in_vmem(energy))
+    return mine, other
 
 
 def coupling_kernel(directions_ref, out_ref, board_ref):
@@ -506,9 +547,12 @@
     def iterate(_, carry):
         inner, curved = carry
         now = resid[...]
-        scaled = jnp.zeros((64, 128), f32)
+        sums = [jnp.zeros((8, 128), f32) for _ in range(8)]
         for k in range(64):
-            scaled = scaled + inverse[k] * resid[k : k + 1, :]
+            line = sub_bcast(now[k // 8 * 8 : k // 8 * 8 + 8, :], k % 8)
+            for c in range(8):
+                sums[c] = sums[c] + inverse[k, 8 * c : 8 * c + 8, :] * line
+        scaled = jnp.concatenate(sums, axis=0)
         mixed = jnp.dot(scaled, mixing, precision=highest, preferred_element_type=f32)
         image = now + power * mixed
         old_mapped = mapped[...]

time: 62.9 us -> 69.1 us (1.099)
  local copies, waits for them, and re-layouts: 0 us -> 5.62 us
  starting transfers between devices: 13.3 us -> 7.89 us
  Pallas kernels: 22.5 us -> 27.8 us
  blocking collectives: 19.3 us -> 23.4 us
  waiting for transfers between devices: 6.49 us -> 3.05 us
    unnamed x0 -> x10, local copies, waits for them, and re-layouts: none -> 5.62 us
    pallas_call x1 -> x2, Pallas kernels: 3.88 us -> 9.24 us  [the longest x1 8.44 us: gram_parts(): pl.pallas_call(gram_kernel, in_specs=[smem, smem, pl.BlockSpec(memory_spa...]
    all_to_all x1, blocking collectives: 19.3 us -> 23.4 us  [body(): lax.all_to_all(sent, AXES, 0, 0, tiled=True, axis_index_groups=groups)]
    ppermute x1, starting transfers between devices: 4.76 us -> 1.47 us  [body(): got = lax.ppermute(other, 'toa', [(u, u ^ 1) for u in range(8)])]
    ppermute x3, waiting for transfers between devices: 3.35 us -> 0.71 us  [body(): lax.ppermute(part, 'toa', [(u, (u + 2 * s) % 8) for u in range(8)])]
    ppermute x3, starting transfers between devices: 5.89 us -> 4.21 us  [body(): lax.ppermute(part, 'toa', [(u, (u + 2 * s) % 8) for u in range(8)])]
    ppermute x1, waiting for transfers between devices: 1.56 us -> 0.75 us  [body(): got = lax.ppermute(other, 'toa', [(u, u ^ 1) for u in range(8)])]
  transfers between devices with their start and end apart: 5 -> 5, of which waited for: 4 -> 3; matrix products, arithmetic and copies ran while one was open for 0% -> 0% of each run, Pallas kernels for 8% -> 9%
where the time goes in v4:
time: 69.1 us; the launch traced here: 68.7 us
  Pallas kernels  27.8 us (40%)
  blocking collectives  23.4 us (34%)
  starting transfers between devices  7.89 us (11%)
  local copies, waits for them, and re-layouts  5.62 us (8%)
  waiting for transfers between devices  3.05 us (4%)
  between operations  0.85 us (1%)
    all_to_all x1, blocking collectives, body(): lax.all_to_all(sent, AXES, 0, 0, tiled=True, axis_index_groups=groups)  23.4 us
    pallas_call x1, Pallas kernels, gram_parts(): pl.pallas_call(gram_kernel, in_specs=[smem, smem, pl.BlockSpec(memory_spa...  8.44 us
    pallas_call x1, Pallas kernels, own_terms(): pl.pallas_call(own_kernel, in_specs=[vmem] * 8, out_specs=[vmem, vmem, sm...  7.49 us
    pallas_call x1, Pallas kernels, conjugate(): pl.pallas_call(gradient_kernel, in_specs=[vmem] * 5, out_specs=[vmem, sme...  5.75 us
    unnamed x10, local copies, waits for them, and re-layouts  5.62 us
    pallas_call x1, Pallas kernels, coupling_inverse(): pl.pallas_call(coupling_kernel, in_specs=[pl.BlockSpec(memory_space=pltpu...  5.3 us
    ppermute x3, starting transfers between devices, body(): lax.ppermute(part, 'toa', [(u, (u + 2 * s) % 8) for u in range(8)])  4.21 us
    ppermute x1, starting transfers between devices, body(): far = lax.ppermute(near, 'toa', [(u, u ^ 1) for u in range(8)])  2.21 us
  transfers between devices with their start and end apart: 5, of which 3 were waited for; matrix products, arithmetic and copies ran while one was open for 0% of the time, Pallas kernels for 9%

profile of v4, /device:TPU:1, one launch (start us, length us, event | category | flops | bytes accessed | tf_op | source)
XLA Modules:
  0.0 68.7 jit_solution(6255848461132006842)
XLA Ops:
  0.6 0.0 copy-start
  0.6 2.8 %copy-done = bf16[96,128,256]{2,1,0:T(8,128)(2,1)S(1)} copy-done((bf16[96,128,256]{2,1,0:T(8,128)(2,1)S(1)}, bf16[96,128,256]{2,1,0:T(8,128)(2,1)}, u32[]{:S(2)}) %copy-start) | copy-done | bytes 6291480
  3.4 0.0 copy-start.1
  3.4 0.8 %copy-done.1 = f32[96,128]{1,0:T(8,128)S(1)} copy-done((f32[96,128]{1,0:T(8,128)S(1)}, f32[96,128]{1,0:T(8,128)}, u32[]{:S(2)}) %copy-start.1) | copy-done | bytes 49176
  4.2 0.7 %copy-done.2 = bf16[96,128]{1,0:T(8,128)(2,1)S(1)} copy-done((bf16[96,128]{1,0:T(8,128)(2,1)S(1)}, bf16[96,128]{1,0:T(8,128)(2,1)}, u32[]{:S(2)}) %copy-start.2) | copy-done | bytes 24600
  5.0 0.0 copy-start.3
  5.0 0.7 copy-done.3
  5.6 0.7 copy-done.4
  6.3 8.4 %gram.1 = (f32[4,264,128]{2,1,0:T(8,128)S(1)}, f32[8,256,256]{2,1,0:T(8,128)S(1)}, f32[8,256,128]{2,1,0:T(8,128)S(1)}, f32[8,128]{1,0:T(8,128)S(1)}, s32[8]{0:T(128)S(1)}) custom-call(s32[96]{0:T(128)S(1)} %copy-done.3, s32[96]{0:T(128)S(1)} %copy-done.4, bf16[96,128,256]{2,1,0:T(8,128)(2,1)S(1)} %copy-done, f32[96,128]{1,0:T(8,128)S(1)} %copy-done.1, ...), custom_call_target="tpu_custom_call" | custom-call | tf_op jit(solution)/shard_map/gram/pallas_call | solution.py:282
  14.7 1.5 %collective-permute-start = (f32[4,264,128]{2,1,0:T(8,128)S(1)}, f32[4,264,128]{2,1,0:T(8,128)S(1)}, u32[]{:S(2)}, u32[]{:S(2)}) collective-permute-start(f32[4,264,128]{2,1,0:T(8,128)S(1)} %get-tuple-element.17), channel_id=1, source_target_pairs={{0,1},{1,0},{2,3},{3,2},{4,5},{5,4},{6,7},{7,6},{8,9},{9,8},{10,11... | collective-permute-start | bytes 1622024 | tf_op jit(solution)/shard_map/ppermute | solution.py:612
  16.2 0.8 %keep.1.kept = f32[4,264,128]{2,1,0:T(8,128)S(1)} custom-call(s32[8]{0:T(128)S(1)} %get-tuple-element.13.counts, f32[8,256,256]{2,1,0:T(8,128)S(1)} %get-tuple-element.14.gram, f32[8,256,128]{2,1,0:T(8,128)S(1)} %get-tuple-element.15.fit, f32[8,128]{1,0:T(8,128)S(1)} %get-tuple-element.16.energy), custom_call_target="tpu_custom_call" | custom-call | tf_op jit(solution)/shard_map/keep/pallas_call | solution.py:302
  17.0 0.8 %collective-permute-done.part0 = f32[4,264,128]{2,1,0:T(8,128)S(1)} collective-permute-done((f32[4,264,128]{2,1,0:T(8,128)S(1)}, f32[4,264,128]{2,1,0:T(8,128)S(1)}, u32[]{:S(2)}, u32[]{:S(2)}) %collective-permute-start) | collective-permute-done | bytes 540704 | tf_op jit(solution)/shard_map/ppermute | solution.py:612
  17.8 1.7 %collective-permute-start.1 = (f32[264,128]{1,0:T(8,128)S(1)}, f32[264,128]{1,0:T(8,128)S(1)}, u32[]{:S(2)}, u32[]{:S(2)}) collective-permute-start(f32[264,128]{1,0:T(8,128)S(1)} %get-tuple-element.25), channel_id=1, source_target_pairs={{0,2},{1,3},{2,4},{3,5},{4,6},{5,7},{6,0},{7,1},{8,10},{9,11},{10,... | collective-permute-start | bytes 405512 | tf_op jit(solution)/shard_map/ppermute | solution.py:616
  19.5 2.1 %collective-permute-start.2 = (f32[264,128]{1,0:T(8,128)S(1)}, f32[264,128]{1,0:T(8,128)S(1)}, u32[]{:S(2)}, u32[]{:S(2)}) collective-permute-start(f32[264,128]{1,0:T(8,128)S(1)} %get-tuple-element.24), channel_id=1, source_target_pairs={{0,4},{1,5},{2,6},{3,7},{4,0},{5,1},{6,2},{7,3},{8,12},{9,13},{10,... | collective-permute-start | bytes 405512 | tf_op jit(solution)/shard_map/ppermute | solution.py:616
  21.6 0.4 collective-permute-start.3
  22.0 5.3 %coupling.1.coupling_ref = f32[128,128]{1,0:T(8,128)S(1)} custom-call(f32[3,128]{1,0:T(4,128)} %directions_ref.1), custom_call_target="tpu_custom_call" | custom-call | tf_op jit(solution)/shard_map/coupling/pallas_call | solution.py:340
  27.3 0.0 collective-permute-done.1.part1
  27.3 0.7 %collective-permute-done.2.part2 = f32[264,128]{1,0:T(8,128)S(1)} collective-permute-done((f32[264,128]{1,0:T(8,128)S(1)}, f32[264,128]{1,0:T(8,128)S(1)}, u32[]{:S(2)}, u32[]{:S(2)}) %collective-permute-start.2) | collective-permute-done | bytes 135200 | tf_op jit(solution)/shard_map/ppermute | solution.py:616
  28.0 0.0 collective-permute-done.3.part3
  28.0 7.5 %own.1 = (f32[1088,128]{1,0:T(8,128)S(1)}, f32[8,128]{1,0:T(8,128)S(1)}, f32[1]{0:T(128)}) custom-call(f32[4,264,128]{2,1,0:T(8,128)S(1)} %keep.1.kept, f32[4,264,128]{2,1,0:T(8,128)S(1)} %collective-permute-done.part0, f32[264,128]{1,0:T(8,128)S(1)} %collective-permute-done.1.part1, f32[264,128]{1,0:T(8,128)S(1)} %collective-permute-done.2.part2, ...), custom_call_target="tpu_custom_call" | custom-call | tf_op jit(solution)/shard_map/own/pallas_call | solution.py:474
  35.5 23.4 %all_to_all.5 = f32[64,1,2176]{2,1,0:T(1,128)S(1)} all-to-all(f32[64,1,2176]{2,1,0:T(1,128)S(1)} %bitcast.11), channel_id=1, replica_groups={{0,2,4,6,8,10,12,14,16,18,20,22,24,26,28,30,32,34,36,38,40,42,44,46,48,..., dimensions={0} | all-to-all | bytes 1114112 | tf_op jit(solution)/shard_map/all_to_all | solution.py:621
  59.0 2.2 %collective-permute-start.4 = (f32[1088,128]{1,0:T(8,128)S(1)}, f32[1088,128]{1,0:T(8,128)S(1)}, u32[]{:S(2)}, u32[]{:S(2)}) collective-permute-start(f32[1088,128]{1,0:T(8,128)S(1)} %bitcast.9), channel_id=1, source_target_pairs={{0,1},{1,0},{2,3},{3,2},{4,5},{5,4},{6,7},{7,6},{8,9},{9,8},{10,11... | collective-permute-start | bytes 1671176 | tf_op jit(solution)/shard_map/ppermute | solution.py:623
  61.2 1.6 %collective-permute-done.4.far_ref = f32[1088,128]{1,0:T(8,128)S(1)} collective-permute-done((f32[1088,128]{1,0:T(8,128)S(1)}, f32[1088,128]{1,0:T(8,128)S(1)}, u32[]{:S(2)}, u32[]{:S(2)}) %collective-permute-start.4) | collective-permute-done | bytes 557088 | tf_op jit(solution)/shard_map/ppermute | solution.py:623
  62.8 5.8 %gradient.1 = (f32[1,64]{1,0:T(1,128)}, f32[1]{0:T(128)}) custom-call(f32[1088,128]{1,0:T(8,128)S(1)} %bitcast.10, f32[1088,128]{1,0:T(8,128)S(1)} %collective-permute-done.4.far_ref, f32[128,128]{1,0:T(8,128)S(1)} %coupling.1.coupling_ref, f32[1,32]{1,0:T(1,128)} %bitcast.13, f32[8,128]{1,0:T(8,128)S(1)} %get-tuple-element.19.extra_ref), custom_call_target="tpu_custom_call" | custom-call | tf_op jit(solution)/shard_map/gradient/pallas_call | solution.py:589
  (3 shorter events, 0.0 us)
Async XLA Ops:
  0.6 2.8 %copy-start = (bf16[96,128,256]{2,1,0:T(8,128)(2,1)S(1)}, bf16[96,128,256]{2,1,0:T(8,128)(2,1)}, u32[]{:S(2)}) copy-start(bf16[96,128,256]{2,1,0:T(8,128)(2,1)} %design_ref.1) | copy-start | bytes 18874372
  3.4 0.8 %copy-start.1 = (f32[96,128]{1,0:T(8,128)S(1)}, f32[96,128]{1,0:T(8,128)}, u32[]{:S(2)}) copy-start(f32[96,128]{1,0:T(8,128)} %weight_ref.1) | copy-start | bytes 147460
  4.2 0.7 %copy-start.2 = (bf16[96,128]{1,0:T(8,128)(2,1)S(1)}, bf16[96,128]{1,0:T(8,128)(2,1)}, u32[]{:S(2)}) copy-start(bf16[96,128]{1,0:T(8,128)(2,1)} %resid_ref.1) | copy-start | bytes 73732
  5.0 0.7 copy-start.3
  5.6 0.7 copy-start.4
  14.7 3.0 %collective-permute-start = (f32[4,264,128]{2,1,0:T(8,128)S(1)}, f32[4,264,128]{2,1,0:T(8,128)S(1)}, u32[]{:S(2)}, u32[]{:S(2)}) collective-permute-start(f32[4,264,128]{2,1,0:T(8,128)S(1)} %get-tuple-element.17), channel_id=1, source_target_pairs={{0,1},{1,0},{2,3},{3,2},{4,5},{5,4},{6,7},{7,6},{8,9},{9,8},{10,11... | collective-permute-start | bytes 1622024 | tf_op jit(solution)/shard_map/ppermute | solution.py:612
  17.8 9.5 %collective-permute-start.1 = (f32[264,128]{1,0:T(8,128)S(1)}, f32[264,128]{1,0:T(8,128)S(1)}, u32[]{:S(2)}, u32[]{:S(2)}) collective-permute-start(f32[264,128]{1,0:T(8,128)S(1)} %get-tuple-element.25), channel_id=1, source_target_pairs={{0,2},{1,3},{2,4},{3,5},{4,6},{5,7},{6,0},{7,1},{8,10},{9,11},{10,... | collective-permute-start | bytes 405512 | tf_op jit(solution)/shard_map/ppermute | solution.py:616
  19.5 8.5 %collective-permute-start.2 = (f32[264,128]{1,0:T(8,128)S(1)}, f32[264,128]{1,0:T(8,128)S(1)}, u32[]{:S(2)}, u32[]{:S(2)}) collective-permute-start(f32[264,128]{1,0:T(8,128)S(1)} %get-tuple-element.24), channel_id=1, source_target_pairs={{0,4},{1,5},{2,6},{3,7},{4,0},{5,1},{6,2},{7,3},{8,12},{9,13},{10,... | collective-permute-start | bytes 405512 | tf_op jit(solution)/shard_map/ppermute | solution.py:616
  21.6 6.4 %collective-permute-start.3 = (f32[264,128]{1,0:T(8,128)S(1)}, f32[264,128]{1,0:T(8,128)S(1)}, u32[]{:S(2)}, u32[]{:S(2)}) collective-permute-start(f32[264,128]{1,0:T(8,128)S(1)} %get-tuple-element.23), channel_id=1, source_target_pairs={{0,6},{1,7},{2,0},{3,1},{4,2},{5,3},{6,4},{7,5},{8,14},{9,15},{10,... | collective-permute-start | bytes 405512 | tf_op jit(solution)/shard_map/ppermute | solution.py:616
  59.0 3.8 %collective-permute-start.4 = (f32[1088,128]{1,0:T(8,128)S(1)}, f32[1088,128]{1,0:T(8,128)S(1)}, u32[]{:S(2)}, u32[]{:S(2)}) collective-permute-start(f32[1088,128]{1,0:T(8,128)S(1)} %bitcast.9), channel_id=1, source_target_pairs={{0,1},{1,0},{2,3},{3,2},{4,5},{5,4},{6,7},{7,6},{8,9},{9,8},{10,11... | collective-permute-start | bytes 1671176 | tf_op jit(solution)/shard_map/ppermute | solution.py:623

commit v5 on v3

--- a/solution.py
+++ b/solution.py
@@ -4,6 +4,7 @@
 from jax.experimental import pallas as pl
 from jax.experimental.pallas import tpu as pltpu
 from jax.sharding import PartitionSpec as P
+
 
 GROUP_PULSARS = 8
 ITERS = 8
@@ -506,9 +507,12 @@
     def iterate(_, carry):
         inner, curved = carry
         now = resid[...]
-        scaled = jnp.zeros((64, 128), f32)
+        sums = [jnp.zeros((8, 128), f32) for _ in range(8)]
         for k in range(64):
-            scaled = scaled + inverse[k] * resid[k : k + 1, :]
+            line = sub_bcast(now[k // 8 * 8 : k // 8 * 8 + 8, :], k % 8)
+            for c in range(8):
+                sums[c] = sums[c] + inverse[k, 8 * c : 8 * c + 8, :] * line
+        scaled = jnp.concatenate(sums, axis=0)
         mixed = jnp.dot(scaled, mixing, precision=highest, preferred_element_type=f32)
         image = now + power * mixed
         old_mapped = mapped[...]

time: 62.9 us -> 62.9 us (level)
  starting transfers between devices: 13.3 us -> 7.82 us
  Pallas kernels: 22.5 us -> 26.8 us
  blocking collectives: 19.3 us -> 20.7 us
    pallas_call x1, Pallas kernels: 3.88 us -> 8.25 us  [gram_parts(): pl.pallas_call(gram_kernel, in_specs=[smem, smem, hbm, vmem, vmem], out_s...]
    ppermute x1, starting transfers between devices: 4.76 us -> 2 us  [body(): got = lax.ppermute(other, 'toa', [(u, u ^ 1) for u in range(8)])]
    ppermute x3, starting transfers between devices: 5.89 us -> 3.58 us  [body(): lax.ppermute(part, 'toa', [(u, (u + 2 * s) % 8) for u in range(8)])]
    all_to_all x1, blocking collectives: 19.3 us -> 20.7 us  [body(): lax.all_to_all(sent, AXES, 0, 0, tiled=True, axis_index_groups=groups)]
where the time goes in v5:
time: 62.9 us; the launch traced here: 62.7 us
  Pallas kernels  26.8 us (43%)
  blocking collectives  20.7 us (33%)
  starting transfers between devices  7.82 us (12%)
  waiting for transfers between devices  6.49 us (10%)
  between operations  0.83 us (1%)
    all_to_all x1, blocking collectives, body(): lax.all_to_all(sent, AXES, 0, 0, tiled=True, axis_index_groups=groups)  20.7 us
    pallas_call x1, Pallas kernels, gram_parts(): pl.pallas_call(gram_kernel, in_specs=[smem, smem, hbm, vmem, vmem], out_s...  8.25 us
    pallas_call x1, Pallas kernels, own_terms(): pl.pallas_call(own_kernel, in_specs=[vmem] * 8, out_specs=[vmem, vmem, sm...  7.48 us
    pallas_call x1, Pallas kernels, conjugate(): pl.pallas_call(gradient_kernel, in_specs=[vmem] * 5, out_specs=[vmem, sme...  5.75 us
    pallas_call x1, Pallas kernels, coupling_inverse(): pl.pallas_call(coupling_kernel, in_specs=[pl.BlockSpec(memory_space=pltpu...  5.3 us
    ppermute x3, starting transfers between devices, body(): lax.ppermute(part, 'toa', [(u, (u + 2 * s) % 8) for u in range(8)])  3.58 us
    ppermute x3, waiting for transfers between devices, body(): lax.ppermute(part, 'toa', [(u, (u + 2 * s) % 8) for u in range(8)])  3.35 us
    ppermute x1, starting transfers between devices, body(): far = lax.ppermute(near, 'toa', [(u, u ^ 1) for u in range(8)])  2.25 us
  transfers between devices with their start and end apart: 5, of which 4 were waited for; matrix products, arithmetic and copies ran while one was open for 0% of the time, Pallas kernels for 8%

profile of v5, /device:TPU:1, one launch (start us, length us, event | category | flops | bytes accessed | tf_op | source)
XLA Modules:
  0.0 62.7 jit_solution(9492904610768026871)
XLA Ops:
  0.6 8.3 %gram.1 = (f32[4,264,128]{2,1,0:T(8,128)S(1)}, f32[4,264,128]{2,1,0:T(8,128)S(1)}) custom-call(s32[96]{0:T(128)} %pulsar_ref.1, s32[96]{0:T(128)} %rows_ref.1, bf16[96,128,256]{2,1,0:T(8,128)(2,1)} %design_ref.1, f32[96,128]{1,0:T(8,128)} %weight_ref.1, bf16[96,128]{1,0:T(8,128)(2,1)} %resid_ref.1), custom_call_target="tpu_custom_call" | custom-call | tf_op jit(solution)/shard_map/gram/pallas_call | solution.py:255
  8.9 2.0 %collective-permute-start = (f32[4,264,128]{2,1,0:T(8,128)S(1)}, f32[4,264,128]{2,1,0:T(8,128)S(1)}, u32[]{:S(2)}, u32[]{:S(2)}) collective-permute-start(f32[4,264,128]{2,1,0:T(8,128)S(1)} %get-tuple-element.11), channel_id=1, source_target_pairs={{0,1},{1,0},{2,3},{3,2},{4,5},{5,4},{6,7},{7,6},{8,9},{9,8},{10,11... | collective-permute-start | bytes 1622024 | tf_op jit(solution)/shard_map/ppermute | solution.py:572
  10.9 1.6 %collective-permute-done.part0 = f32[4,264,128]{2,1,0:T(8,128)S(1)} collective-permute-done((f32[4,264,128]{2,1,0:T(8,128)S(1)}, f32[4,264,128]{2,1,0:T(8,128)S(1)}, u32[]{:S(2)}, u32[]{:S(2)}) %collective-permute-start) | collective-permute-done | bytes 540704 | tf_op jit(solution)/shard_map/ppermute | solution.py:572
  12.5 2.9 %collective-permute-start.3 = (f32[264,128]{1,0:T(8,128)S(1)}, f32[264,128]{1,0:T(8,128)S(1)}, u32[]{:S(2)}, u32[]{:S(2)}) collective-permute-start(f32[264,128]{1,0:T(8,128)S(1)} %get-tuple-element.17), channel_id=1, source_target_pairs={{0,6},{1,7},{2,0},{3,1},{4,2},{5,3},{6,4},{7,5},{8,14},{9,15},{10,... | collective-permute-start | bytes 405512 | tf_op jit(solution)/shard_map/ppermute | solution.py:576
  15.4 0.0 collective-permute-start.2
  15.4 0.7 %collective-permute-start.1 = (f32[264,128]{1,0:T(8,128)S(1)}, f32[264,128]{1,0:T(8,128)S(1)}, u32[]{:S(2)}, u32[]{:S(2)}) collective-permute-start(f32[264,128]{1,0:T(8,128)S(1)} %get-tuple-element.19), channel_id=1, source_target_pairs={{0,2},{1,3},{2,4},{3,5},{4,6},{5,7},{6,0},{7,1},{8,10},{9,11},{10,... | collective-permute-start | bytes 405512 | tf_op jit(solution)/shard_map/ppermute | solution.py:576
  16.1 5.3 %coupling.1.coupling_ref = f32[128,128]{1,0:T(8,128)S(1)} custom-call(f32[3,128]{1,0:T(4,128)} %directions_ref.1), custom_call_target="tpu_custom_call" | custom-call | tf_op jit(solution)/shard_map/coupling/pallas_call | solution.py:300
  21.4 0.0 collective-permute-done.3.part3
  21.4 0.1 collective-permute-done.2.part2
  21.5 3.2 %collective-permute-done.1.part1 = f32[264,128]{1,0:T(8,128)S(1)} collective-permute-done((f32[264,128]{1,0:T(8,128)S(1)}, f32[264,128]{1,0:T(8,128)S(1)}, u32[]{:S(2)}, u32[]{:S(2)}) %collective-permute-start.1) | collective-permute-done | bytes 135200 | tf_op jit(solution)/shard_map/ppermute | solution.py:576
  24.7 7.5 %own.1 = (f32[1088,128]{1,0:T(8,128)S(1)}, f32[8,128]{1,0:T(8,128)S(1)}, f32[1]{0:T(128)}) custom-call(f32[4,264,128]{2,1,0:T(8,128)S(1)} %get-tuple-element.10.kept, f32[4,264,128]{2,1,0:T(8,128)S(1)} %collective-permute-done.part0, f32[264,128]{1,0:T(8,128)S(1)} %collective-permute-done.1.part1, f32[264,128]{1,0:T(8,128)S(1)} %collective-permute-done.2.part2, ...), custom_call_target="tpu_custom_call" | custom-call | tf_op jit(solution)/shard_map/own/pallas_call | solution.py:434
  32.2 20.7 %all_to_all.5 = f32[64,1,2176]{2,1,0:T(1,128)S(1)} all-to-all(f32[64,1,2176]{2,1,0:T(1,128)S(1)} %bitcast.11), channel_id=1, replica_groups={{0,2,4,6,8,10,12,14,16,18,20,22,24,26,28,30,32,34,36,38,40,42,44,46,48,..., dimensions={0} | all-to-all | bytes 1114112 | tf_op jit(solution)/shard_map/all_to_all | solution.py:581
  52.9 2.3 %collective-permute-start.4 = (f32[1088,128]{1,0:T(8,128)S(1)}, f32[1088,128]{1,0:T(8,128)S(1)}, u32[]{:S(2)}, u32[]{:S(2)}) collective-permute-start(f32[1088,128]{1,0:T(8,128)S(1)} %bitcast.9), channel_id=1, source_target_pairs={{0,1},{1,0},{2,3},{3,2},{4,5},{5,4},{6,7},{7,6},{8,9},{9,8},{10,11... | collective-permute-start | bytes 1671176 | tf_op jit(solution)/shard_map/ppermute | solution.py:583
  55.2 1.6 %collective-permute-done.4.far_ref = f32[1088,128]{1,0:T(8,128)S(1)} collective-permute-done((f32[1088,128]{1,0:T(8,128)S(1)}, f32[1088,128]{1,0:T(8,128)S(1)}, u32[]{:S(2)}, u32[]{:S(2)}) %collective-permute-start.4) | collective-permute-done | bytes 557088 | tf_op jit(solution)/shard_map/ppermute | solution.py:583
  56.8 5.8 %gradient.1 = (f32[1,64]{1,0:T(1,128)}, f32[1]{0:T(128)}) custom-call(f32[1088,128]{1,0:T(8,128)S(1)} %bitcast.10, f32[1088,128]{1,0:T(8,128)S(1)} %collective-permute-done.4.far_ref, f32[128,128]{1,0:T(8,128)S(1)} %coupling.1.coupling_ref, f32[1,32]{1,0:T(1,128)} %bitcast.13, f32[8,128]{1,0:T(8,128)S(1)} %get-tuple-element.13.extra_ref), custom_call_target="tpu_custom_call" | custom-call | tf_op jit(solution)/shard_map/gradient/pallas_call | solution.py:549
  (1 shorter events, 0.0 us)
Async XLA Ops:
  8.9 3.6 %collective-permute-start = (f32[4,264,128]{2,1,0:T(8,128)S(1)}, f32[4,264,128]{2,1,0:T(8,128)S(1)}, u32[]{:S(2)}, u32[]{:S(2)}) collective-permute-start(f32[4,264,128]{2,1,0:T(8,128)S(1)} %get-tuple-element.11), channel_id=1, source_target_pairs={{0,1},{1,0},{2,3},{3,2},{4,5},{5,4},{6,7},{7,6},{8,9},{9,8},{10,11... | collective-permute-start | bytes 1622024 | tf_op jit(solution)/shard_map/ppermute | solution.py:572
  12.5 8.9 %collective-permute-start.3 = (f32[264,128]{1,0:T(8,128)S(1)}, f32[264,128]{1,0:T(8,128)S(1)}, u32[]{:S(2)}, u32[]{:S(2)}) collective-permute-start(f32[264,128]{1,0:T(8,128)S(1)} %get-tuple-element.17), channel_id=1, source_target_pairs={{0,6},{1,7},{2,0},{3,1},{4,2},{5,3},{6,4},{7,5},{8,14},{9,15},{10,... | collective-permute-start | bytes 405512 | tf_op jit(solution)/shard_map/ppermute | solution.py:576
  15.4 6.1 %collective-permute-start.2 = (f32[264,128]{1,0:T(8,128)S(1)}, f32[264,128]{1,0:T(8,128)S(1)}, u32[]{:S(2)}, u32[]{:S(2)}) collective-permute-start(f32[264,128]{1,0:T(8,128)S(1)} %get-tuple-element.18), channel_id=1, source_target_pairs={{0,4},{1,5},{2,6},{3,7},{4,0},{5,1},{6,2},{7,3},{8,12},{9,13},{10,... | collective-permute-start | bytes 405512 | tf_op jit(solution)/shard_map/ppermute | solution.py:576
  15.4 9.3 %collective-permute-start.1 = (f32[264,128]{1,0:T(8,128)S(1)}, f32[264,128]{1,0:T(8,128)S(1)}, u32[]{:S(2)}, u32[]{:S(2)}) collective-permute-start(f32[264,128]{1,0:T(8,128)S(1)} %get-tuple-element.19), channel_id=1, source_target_pairs={{0,2},{1,3},{2,4},{3,5},{4,6},{5,7},{6,0},{7,1},{8,10},{9,11},{10,... | collective-permute-start | bytes 405512 | tf_op jit(solution)/shard_map/ppermute | solution.py:576
  52.9 3.8 %collective-permute-start.4 = (f32[1088,128]{1,0:T(8,128)S(1)}, f32[1088,128]{1,0:T(8,128)S(1)}, u32[]{:S(2)}, u32[]{:S(2)}) collective-permute-start(f32[1088,128]{1,0:T(8,128)S(1)} %bitcast.9), channel_id=1, source_target_pairs={{0,1},{1,0},{2,3},{3,2},{4,5},{5,4},{6,7},{7,6},{8,9},{9,8},{10,11... | collective-permute-start | bytes 1671176 | tf_op jit(solution)/shard_map/ppermute | solution.py:583

commit v6 on v5

--- a/solution.py
+++ b/solution.py
@@ -445,6 +445,14 @@
     )(*map(in_vmem, parts), own_prior, spectrum, in_vmem(coupling))
 
 
+def three_parts(value):
+    high = value.astype(jnp.bfloat16)
+    rest = value - high.astype(f32)
+    middle = rest.astype(jnp.bfloat16)
+    low = (rest - middle.astype(f32)).astype(jnp.bfloat16)
+    return high, middle, low
+
+
 def gradient_kernel(
     near_ref,
     far_ref,
@@ -456,7 +464,7 @@
     flat,
     inverse,
     target,
-    resid,
+    weights,
     direction,
     mapped,
     answer,
@@ -499,21 +507,25 @@
     row, col = iota((128, 128), 0), iota((128, 128), 1)
     mixing = jnp.where(row == col, 0.0, coupling_ref[...])
     power = power_column(spectrum_ref)
-    resid[...] = target[...]
+    power = jnp.broadcast_to(power, (64, 128))
     direction[...] = jnp.zeros((64, 128), f32)
     mapped[...] = jnp.zeros((64, 128), f32)
     answer[...] = jnp.zeros((64, 128), f32)
+    high, middle, low = three_parts(mixing)
+    weights[...] = jnp.concatenate([high, middle, high, middle, low, high], axis=0)
 
     def iterate(_, carry):
-        inner, curved = carry
-        now = resid[...]
+        inner, curved, *rows = carry
         sums = [jnp.zeros((8, 128), f32) for _ in range(8)]
         for k in range(64):
-            line = sub_bcast(now[k // 8 * 8 : k // 8 * 8 + 8, :], k % 8)
+            line = sub_bcast(rows[k // 8], k % 8)
             for c in range(8):
                 sums[c] = sums[c] + inverse[k, 8 * c : 8 * c + 8, :] * line
+        now = jnp.concatenate(rows, axis=0)
         scaled = jnp.concatenate(sums, axis=0)
-        mixed = jnp.dot(scaled, mixing, precision=highest, preferred_element_type=f32)
+        high, middle, low = three_parts(scaled)
+        wide = jnp.concatenate([high, high, middle, middle, high, low], axis=1)
+        mixed = jnp.dot(wide, weights[...], preferred_element_type=f32)
         image = now + power * mixed
         old_mapped = mapped[...]
         inner_next = total(now * scaled)
@@ -527,10 +539,11 @@
         direction[...] = toward
         mapped[...] = image
         answer[...] = answer[...] + step * toward
-        resid[...] = now - step * image
-        return inner_next, curved
-
-    lax.fori_loop(0, ITERS, iterate, (jnp.ones((1, 1), f32), jnp.zeros((1, 1), f32)))
+        now = now - step * image
+        return (inner_next, curved, *[now[8 * c : 8 * c + 8, :] for c in range(8)])
+
+    first = [target[8 * c : 8 * c + 8, :] for c in range(8)]
+    lax.fori_loop(0, ITERS, iterate, (jnp.ones((1, 1), f32), jnp.zeros((1, 1), f32), *first))
     _, _, own = location()
     value = answer[...]
     gained = jnp.sum(target[...] * value, axis=0, keepdims=True)
@@ -555,7 +568,7 @@
             pltpu.VMEM((WIDTH, 128), f32),
             pltpu.VMEM((64, 64, 128), f32),
             square,
-            square,
+            pltpu.VMEM((6 * 128, 128), jnp.bfloat16),
             square,
             square,
             square,

time: 62.9 us -> 62.4 us (level)
  transfers between devices with their start and end apart: 5 -> 5, of which waited for: 4 -> 4; matrix products, arithmetic and copies ran while one was open for 0% -> 0% of each run, Pallas kernels for 8% -> 9%
where the time goes in v6:
time: 62.4 us; the launch traced here: 62.2 us
  Pallas kernels  26.2 us (42%)
  blocking collectives  20.7 us (33%)
  starting transfers between devices  7.82 us (13%)
  waiting for transfers between devices  6.49 us (10%)
  between operations  0.83 us (1%)
    all_to_all x1, blocking collectives, body(): lax.all_to_all(sent, AXES, 0, 0, tiled=True, axis_index_groups=groups)  20.7 us
    pallas_call x1, Pallas kernels, gram_parts(): pl.pallas_call(gram_kernel, in_specs=[smem, smem, hbm, vmem, vmem], out_s...  8.25 us
    pallas_call x1, Pallas kernels, own_terms(): pl.pallas_call(own_kernel, in_specs=[vmem] * 8, out_specs=[vmem, vmem, sm...  7.48 us
    pallas_call x1, Pallas kernels, coupling_inverse(): pl.pallas_call(coupling_kernel, in_specs=[pl.BlockSpec(memory_space=pltpu...  5.3 us
    pallas_call x1, Pallas kernels, conjugate(): pl.pallas_call(gradient_kernel, in_specs=[vmem] * 5, out_specs=[vmem, sme...  5.22 us
    ppermute x3, starting transfers between devices, body(): lax.ppermute(part, 'toa', [(u, (u + 2 * s) % 8) for u in range(8)])  3.58 us
    ppermute x3, waiting for transfers between devices, body(): lax.ppermute(part, 'toa', [(u, (u + 2 * s) % 8) for u in range(8)])  3.35 us
    ppermute x1, starting transfers between devices, body(): far = lax.ppermute(near, 'toa', [(u, u ^ 1) for u in range(8)])  2.25 us
  transfers between devices with their start and end apart: 5, of which 4 were waited for; matrix products, arithmetic and copies ran while one was open for 0% of the time, Pallas kernels for 9%

profile of v6, /device:TPU:1, one launch (start us, length us, event | category | flops | bytes accessed | tf_op | source)
XLA Modules:
  0.0 62.2 jit_solution(5663847526907675736)
XLA Ops:
  0.6 8.3 %gram.1 = (f32[4,264,128]{2,1,0:T(8,128)S(1)}, f32[4,264,128]{2,1,0:T(8,128)S(1)}) custom-call(s32[96]{0:T(128)} %pulsar_ref.1, s32[96]{0:T(128)} %rows_ref.1, bf16[96,128,256]{2,1,0:T(8,128)(2,1)} %design_ref.1, f32[96,128]{1,0:T(8,128)} %weight_ref.1, bf16[96,128]{1,0:T(8,128)(2,1)} %resid_ref.1), custom_call_target="tpu_custom_call" | custom-call | tf_op jit(solution)/shard_map/gram/pallas_call | solution.py:255
  8.9 2.0 %collective-permute-start = (f32[4,264,128]{2,1,0:T(8,128)S(1)}, f32[4,264,128]{2,1,0:T(8,128)S(1)}, u32[]{:S(2)}, u32[]{:S(2)}) collective-permute-start(f32[4,264,128]{2,1,0:T(8,128)S(1)} %get-tuple-element.11), channel_id=1, source_target_pairs={{0,1},{1,0},{2,3},{3,2},{4,5},{5,4},{6,7},{7,6},{8,9},{9,8},{10,11... | collective-permute-start | bytes 1622024 | tf_op jit(solution)/shard_map/ppermute | solution.py:585
  10.9 1.6 %collective-permute-done.part0 = f32[4,264,128]{2,1,0:T(8,128)S(1)} collective-permute-done((f32[4,264,128]{2,1,0:T(8,128)S(1)}, f32[4,264,128]{2,1,0:T(8,128)S(1)}, u32[]{:S(2)}, u32[]{:S(2)}) %collective-permute-start) | collective-permute-done | bytes 540704 | tf_op jit(solution)/shard_map/ppermute | solution.py:585
  12.5 2.9 %collective-permute-start.3 = (f32[264,128]{1,0:T(8,128)S(1)}, f32[264,128]{1,0:T(8,128)S(1)}, u32[]{:S(2)}, u32[]{:S(2)}) collective-permute-start(f32[264,128]{1,0:T(8,128)S(1)} %get-tuple-element.17), channel_id=1, source_target_pairs={{0,6},{1,7},{2,0},{3,1},{4,2},{5,3},{6,4},{7,5},{8,14},{9,15},{10,... | collective-permute-start | bytes 405512 | tf_op jit(solution)/shard_map/ppermute | solution.py:589
  15.4 0.0 collective-permute-start.2
  15.4 0.7 %collective-permute-start.1 = (f32[264,128]{1,0:T(8,128)S(1)}, f32[264,128]{1,0:T(8,128)S(1)}, u32[]{:S(2)}, u32[]{:S(2)}) collective-permute-start(f32[264,128]{1,0:T(8,128)S(1)} %get-tuple-element.19), channel_id=1, source_target_pairs={{0,2},{1,3},{2,4},{3,5},{4,6},{5,7},{6,0},{7,1},{8,10},{9,11},{10,... | collective-permute-start | bytes 405512 | tf_op jit(solution)/shard_map/ppermute | solution.py:589
  16.1 5.3 %coupling.1.coupling_ref = f32[128,128]{1,0:T(8,128)S(1)} custom-call(f32[3,128]{1,0:T(4,128)} %directions_ref.1), custom_call_target="tpu_custom_call" | custom-call | tf_op jit(solution)/shard_map/coupling/pallas_call | solution.py:300
  21.4 0.0 collective-permute-done.3.part3
  21.4 0.1 collective-permute-done.2.part2
  21.5 3.2 %collective-permute-done.1.part1 = f32[264,128]{1,0:T(8,128)S(1)} collective-permute-done((f32[264,128]{1,0:T(8,128)S(1)}, f32[264,128]{1,0:T(8,128)S(1)}, u32[]{:S(2)}, u32[]{:S(2)}) %collective-permute-start.1) | collective-permute-done | bytes 135200 | tf_op jit(solution)/shard_map/ppermute | solution.py:589
  24.7 7.5 %own.1 = (f32[1088,128]{1,0:T(8,128)S(1)}, f32[8,128]{1,0:T(8,128)S(1)}, f32[1]{0:T(128)}) custom-call(f32[4,264,128]{2,1,0:T(8,128)S(1)} %get-tuple-element.10.kept, f32[4,264,128]{2,1,0:T(8,128)S(1)} %collective-permute-done.part0, f32[264,128]{1,0:T(8,128)S(1)} %collective-permute-done.1.part1, f32[264,128]{1,0:T(8,128)S(1)} %collective-permute-done.2.part2, ...), custom_call_target="tpu_custom_call" | custom-call | tf_op jit(solution)/shard_map/own/pallas_call | solution.py:434
  32.2 20.7 %all_to_all.5 = f32[64,1,2176]{2,1,0:T(1,128)S(1)} all-to-all(f32[64,1,2176]{2,1,0:T(1,128)S(1)} %bitcast.11), channel_id=1, replica_groups={{0,2,4,6,8,10,12,14,16,18,20,22,24,26,28,30,32,34,36,38,40,42,44,46,48,..., dimensions={0} | all-to-all | bytes 1114112 | tf_op jit(solution)/shard_map/all_to_all | solution.py:594
  52.9 2.3 %collective-permute-start.4 = (f32[1088,128]{1,0:T(8,128)S(1)}, f32[1088,128]{1,0:T(8,128)S(1)}, u32[]{:S(2)}, u32[]{:S(2)}) collective-permute-start(f32[1088,128]{1,0:T(8,128)S(1)} %bitcast.9), channel_id=1, source_target_pairs={{0,1},{1,0},{2,3},{3,2},{4,5},{5,4},{6,7},{7,6},{8,9},{9,8},{10,11... | collective-permute-start | bytes 1671176 | tf_op jit(solution)/shard_map/ppermute | solution.py:596
  55.2 1.6 %collective-permute-done.4.far_ref = f32[1088,128]{1,0:T(8,128)S(1)} collective-permute-done((f32[1088,128]{1,0:T(8,128)S(1)}, f32[1088,128]{1,0:T(8,128)S(1)}, u32[]{:S(2)}, u32[]{:S(2)}) %collective-permute-start.4) | collective-permute-done | bytes 557088 | tf_op jit(solution)/shard_map/ppermute | solution.py:596
  56.8 5.2 %gradient.1 = (f32[1,64]{1,0:T(1,128)}, f32[1]{0:T(128)}) custom-call(f32[1088,128]{1,0:T(8,128)S(1)} %bitcast.10, f32[1088,128]{1,0:T(8,128)S(1)} %collective-permute-done.4.far_ref, f32[128,128]{1,0:T(8,128)S(1)} %coupling.1.coupling_ref, f32[1,32]{1,0:T(1,128)} %bitcast.13, f32[8,128]{1,0:T(8,128)S(1)} %get-tuple-element.13.extra_ref), custom_call_target="tpu_custom_call" | custom-call | tf_op jit(solution)/shard_map/gradient/pallas_call | solution.py:562
  (1 shorter events, 0.0 us)
Async XLA Ops:
  8.9 3.6 %collective-permute-start = (f32[4,264,128]{2,1,0:T(8,128)S(1)}, f32[4,264,128]{2,1,0:T(8,128)S(1)}, u32[]{:S(2)}, u32[]{:S(2)}) collective-permute-start(f32[4,264,128]{2,1,0:T(8,128)S(1)} %get-tuple-element.11), channel_id=1, source_target_pairs={{0,1},{1,0},{2,3},{3,2},{4,5},{5,4},{6,7},{7,6},{8,9},{9,8},{10,11... | collective-permute-start | bytes 1622024 | tf_op jit(solution)/shard_map/ppermute | solution.py:585
  12.5 8.9 %collective-permute-start.3 = (f32[264,128]{1,0:T(8,128)S(1)}, f32[264,128]{1,0:T(8,128)S(1)}, u32[]{:S(2)}, u32[]{:S(2)}) collective-permute-start(f32[264,128]{1,0:T(8,128)S(1)} %get-tuple-element.17), channel_id=1, source_target_pairs={{0,6},{1,7},{2,0},{3,1},{4,2},{5,3},{6,4},{7,5},{8,14},{9,15},{10,... | collective-permute-start | bytes 405512 | tf_op jit(solution)/shard_map/ppermute | solution.py:589
  15.4 6.1 %collective-permute-start.2 = (f32[264,128]{1,0:T(8,128)S(1)}, f32[264,128]{1,0:T(8,128)S(1)}, u32[]{:S(2)}, u32[]{:S(2)}) collective-permute-start(f32[264,128]{1,0:T(8,128)S(1)} %get-tuple-element.18), channel_id=1, source_target_pairs={{0,4},{1,5},{2,6},{3,7},{4,0},{5,1},{6,2},{7,3},{8,12},{9,13},{10,... | collective-permute-start | bytes 405512 | tf_op jit(solution)/shard_map/ppermute | solution.py:589
  15.4 9.3 %collective-permute-start.1 = (f32[264,128]{1,0:T(8,128)S(1)}, f32[264,128]{1,0:T(8,128)S(1)}, u32[]{:S(2)}, u32[]{:S(2)}) collective-permute-start(f32[264,128]{1,0:T(8,128)S(1)} %get-tuple-element.19), channel_id=1, source_target_pairs={{0,2},{1,3},{2,4},{3,5},{4,6},{5,7},{6,0},{7,1},{8,10},{9,11},{10,... | collective-permute-start | bytes 405512 | tf_op jit(solution)/shard_map/ppermute | solution.py:589
  52.9 3.8 %collective-permute-start.4 = (f32[1088,128]{1,0:T(8,128)S(1)}, f32[1088,128]{1,0:T(8,128)S(1)}, u32[]{:S(2)}, u32[]{:S(2)}) collective-permute-start(f32[1088,128]{1,0:T(8,128)S(1)} %bitcast.9), channel_id=1, source_target_pairs={{0,1},{1,0},{2,3},{3,2},{4,5},{5,4},{6,7},{7,6},{8,9},{9,8},{10,11... | collective-permute-start | bytes 1671176 | tf_op jit(solution)/shard_map/ppermute | solution.py:596

commit v7 on v6

--- a/solution.py
+++ b/solution.py
@@ -465,8 +465,12 @@
     inverse,
     target,
     weights,
+    resid,
+    scale,
     direction,
     mapped,
+    solved,
+    twice,
     answer,
     turned,
 ):
@@ -508,42 +512,63 @@
     mixing = jnp.where(row == col, 0.0, coupling_ref[...])
     power = power_column(spectrum_ref)
     power = jnp.broadcast_to(power, (64, 128))
-    direction[...] = jnp.zeros((64, 128), f32)
-    mapped[...] = jnp.zeros((64, 128), f32)
-    answer[...] = jnp.zeros((64, 128), f32)
+    zero = jnp.zeros((64, 128), f32)
+    for ref in (direction, mapped, solved, twice, answer):
+        ref[...] = zero
     high, middle, low = three_parts(mixing)
     weights[...] = jnp.concatenate([high, middle, high, middle, low, high], axis=0)
 
-    def iterate(_, carry):
-        inner, curved, *rows = carry
+    def applied(rows):
         sums = [jnp.zeros((8, 128), f32) for _ in range(8)]
         for k in range(64):
             line = sub_bcast(rows[k // 8], k % 8)
             for c in range(8):
                 sums[c] = sums[c] + inverse[k, 8 * c : 8 * c + 8, :] * line
-        now = jnp.concatenate(rows, axis=0)
         scaled = jnp.concatenate(sums, axis=0)
         high, middle, low = three_parts(scaled)
         wide = jnp.concatenate([high, high, middle, middle, high, low], axis=1)
         mixed = jnp.dot(wide, weights[...], preferred_element_type=f32)
-        image = now + power * mixed
-        old_mapped = mapped[...]
+        return scaled, jnp.concatenate(rows, axis=0) + power * mixed
+
+    def in_rows(value):
+        return [value[8 * c : 8 * c + 8, :] for c in range(8)]
+
+    def scalars(inner, curved, now, scaled, image):
         inner_next = total(now * scaled)
         straight = total(scaled * image)
-        crossing = total(scaled * old_mapped)
+        crossing = total(scaled * mapped[...])
         ratio = inner_next / inner
         curved = straight + ratio * (2.0 * crossing + ratio * curved)
-        step = inner_next / curved
+        return inner_next, curved, ratio, inner_next / curved
+
+    resid[...] = target[...]
+    first, image = applied(in_rows(target[...]))
+    scale[...] = first
+
+    def iterate(_, carry):
+        inner, curved, *rows = carry
+        image = jnp.concatenate(rows, axis=0)
+        now, scaled = resid[...], scale[...]
+        inner, curved, ratio, step = scalars(inner, curved, now, scaled, image)
+        solved_image, next_image = applied(rows)
         toward = scaled + ratio * direction[...]
-        image = image + ratio * old_mapped
+        along = image + ratio * mapped[...]
+        solved_now = solved_image + ratio * solved[...]
+        twice_now = next_image + ratio * twice[...]
         direction[...] = toward
-        mapped[...] = image
+        mapped[...] = along
+        solved[...] = solved_now
+        twice[...] = twice_now
         answer[...] = answer[...] + step * toward
-        now = now - step * image
-        return (inner_next, curved, *[now[8 * c : 8 * c + 8, :] for c in range(8)])
-
-    first = [target[8 * c : 8 * c + 8, :] for c in range(8)]
-    lax.fori_loop(0, ITERS, iterate, (jnp.ones((1, 1), f32), jnp.zeros((1, 1), f32), *first))
+        resid[...] = now - step * along
+        scale[...] = scaled - step * solved_now
+        return (inner, curved, *in_rows(image - step * twice_now))
+
+    start = (jnp.ones((1, 1), f32), jnp.zeros((1, 1), f32), *in_rows(image))
+    inner, curved, *rows = lax.fori_loop(0, ITERS - 1, iterate, start)
+    image = jnp.concatenate(rows, axis=0)
+    inner, curved, ratio, step = scalars(inner, curved, resid[...], scale[...], image)
+    answer[...] = answer[...] + step * (scale[...] + ratio * direction[...])
     _, _, own = location()
     value = answer[...]
     gained = jnp.sum(target[...] * value, axis=0, keepdims=True)
@@ -569,9 +594,7 @@
             pltpu.VMEM((64, 64, 128), f32),
             square,
             pltpu.VMEM((6 * 128, 128), jnp.bfloat16),
-            square,
-            square,
-            square,
+            *[square] * 7,
             pltpu.VMEM((128, 128), f32),
         ],
         name="gradient",

time: 62.4 us -> 61.7 us (0.989)
    pallas_call x1, Pallas kernels: 5.22 us -> 4.52 us  [conjugate(): pl.pallas_call(gradient_kernel, in_specs=[vmem] * 5, out_specs=[vmem, sme...]
where the time goes in v7:
time: 61.7 us; the launch traced here: 61.5 us
  Pallas kernels  25.6 us (41%)
  blocking collectives  20.7 us (34%)
  starting transfers between devices  7.82 us (13%)
  waiting for transfers between devices  6.49 us (11%)
  between operations  0.83 us (1%)
    all_to_all x1, blocking collectives, body(): lax.all_to_all(sent, AXES, 0, 0, tiled=True, axis_index_groups=groups)  20.7 us
    pallas_call x1, Pallas kernels, gram_parts(): pl.pallas_call(gram_kernel, in_specs=[smem, smem, hbm, vmem, vmem], out_s...  8.25 us
    pallas_call x1, Pallas kernels, own_terms(): pl.pallas_call(own_kernel, in_specs=[vmem] * 8, out_specs=[vmem, vmem, sm...  7.48 us
    pallas_call x1, Pallas kernels, coupling_inverse(): pl.pallas_call(coupling_kernel, in_specs=[pl.BlockSpec(memory_space=pltpu...  5.3 us
    pallas_call x1, Pallas kernels, conjugate(): pl.pallas_call(gradient_kernel, in_specs=[vmem] * 5, out_specs=[vmem, sme...  4.52 us
    ppermute x3, starting transfers between devices, body(): lax.ppermute(part, 'toa', [(u, (u + 2 * s) % 8) for u in range(8)])  3.58 us
    ppermute x3, waiting for transfers between devices, body(): lax.ppermute(part, 'toa', [(u, (u + 2 * s) % 8) for u in range(8)])  3.35 us
    ppermute x1, starting transfers between devices, body(): far = lax.ppermute(near, 'toa', [(u, u ^ 1) for u in range(8)])  2.25 us
  transfers between devices with their start and end apart: 5, of which 4 were waited for; matrix products, arithmetic and copies ran while one was open for 0% of the time, Pallas kernels for 9%

profile of v7, /device:TPU:1, one launch (start us, length us, event | category | flops | bytes accessed | tf_op | source)
XLA Modules:
  0.0 61.5 jit_solution(8695578520707724779)
XLA Ops:
  0.6 8.3 %gram.1 = (f32[4,264,128]{2,1,0:T(8,128)S(1)}, f32[4,264,128]{2,1,0:T(8,128)S(1)}) custom-call(s32[96]{0:T(128)} %pulsar_ref.1, s32[96]{0:T(128)} %rows_ref.1, bf16[96,128,256]{2,1,0:T(8,128)(2,1)} %design_ref.1, f32[96,128]{1,0:T(8,128)} %weight_ref.1, bf16[96,128]{1,0:T(8,128)(2,1)} %resid_ref.1), custom_call_target="tpu_custom_call" | custom-call | tf_op jit(solution)/shard_map/gram/pallas_call | solution.py:255
  8.9 2.0 %collective-permute-start = (f32[4,264,128]{2,1,0:T(8,128)S(1)}, f32[4,264,128]{2,1,0:T(8,128)S(1)}, u32[]{:S(2)}, u32[]{:S(2)}) collective-permute-start(f32[4,264,128]{2,1,0:T(8,128)S(1)} %get-tuple-element.11), channel_id=1, source_target_pairs={{0,1},{1,0},{2,3},{3,2},{4,5},{5,4},{6,7},{7,6},{8,9},{9,8},{10,11... | collective-permute-start | bytes 1622024 | tf_op jit(solution)/shard_map/ppermute | solution.py:608
  10.9 1.6 %collective-permute-done.part0 = f32[4,264,128]{2,1,0:T(8,128)S(1)} collective-permute-done((f32[4,264,128]{2,1,0:T(8,128)S(1)}, f32[4,264,128]{2,1,0:T(8,128)S(1)}, u32[]{:S(2)}, u32[]{:S(2)}) %collective-permute-start) | collective-permute-done | bytes 540704 | tf_op jit(solution)/shard_map/ppermute | solution.py:608
  12.5 2.9 %collective-permute-start.3 = (f32[264,128]{1,0:T(8,128)S(1)}, f32[264,128]{1,0:T(8,128)S(1)}, u32[]{:S(2)}, u32[]{:S(2)}) collective-permute-start(f32[264,128]{1,0:T(8,128)S(1)} %get-tuple-element.17), channel_id=1, source_target_pairs={{0,6},{1,7},{2,0},{3,1},{4,2},{5,3},{6,4},{7,5},{8,14},{9,15},{10,... | collective-permute-start | bytes 405512 | tf_op jit(solution)/shard_map/ppermute | solution.py:612
  15.4 0.0 collective-permute-start.2
  15.4 0.7 %collective-permute-start.1 = (f32[264,128]{1,0:T(8,128)S(1)}, f32[264,128]{1,0:T(8,128)S(1)}, u32[]{:S(2)}, u32[]{:S(2)}) collective-permute-start(f32[264,128]{1,0:T(8,128)S(1)} %get-tuple-element.19), channel_id=1, source_target_pairs={{0,2},{1,3},{2,4},{3,5},{4,6},{5,7},{6,0},{7,1},{8,10},{9,11},{10,... | collective-permute-start | bytes 405512 | tf_op jit(solution)/shard_map/ppermute | solution.py:612
  16.1 5.3 %coupling.1.coupling_ref = f32[128,128]{1,0:T(8,128)S(1)} custom-call(f32[3,128]{1,0:T(4,128)} %directions_ref.1), custom_call_target="tpu_custom_call" | custom-call | tf_op jit(solution)/shard_map/coupling/pallas_call | solution.py:300
  21.4 0.0 collective-permute-done.3.part3
  21.4 0.1 collective-permute-done.2.part2
  21.5 3.2 %collective-permute-done.1.part1 = f32[264,128]{1,0:T(8,128)S(1)} collective-permute-done((f32[264,128]{1,0:T(8,128)S(1)}, f32[264,128]{1,0:T(8,128)S(1)}, u32[]{:S(2)}, u32[]{:S(2)}) %collective-permute-start.1) | collective-permute-done | bytes 135200 | tf_op jit(solution)/shard_map/ppermute | solution.py:612
  24.7 7.5 %own.1 = (f32[1088,128]{1,0:T(8,128)S(1)}, f32[8,128]{1,0:T(8,128)S(1)}, f32[1]{0:T(128)}) custom-call(f32[4,264,128]{2,1,0:T(8,128)S(1)} %get-tuple-element.10.kept, f32[4,264,128]{2,1,0:T(8,128)S(1)} %collective-permute-done.part0, f32[264,128]{1,0:T(8,128)S(1)} %collective-permute-done.1.part1, f32[264,128]{1,0:T(8,128)S(1)} %collective-permute-done.2.part2, ...), custom_call_target="tpu_custom_call" | custom-call | tf_op jit(solution)/shard_map/own/pallas_call | solution.py:434
  32.2 20.7 %all_to_all.5 = f32[64,1,2176]{2,1,0:T(1,128)S(1)} all-to-all(f32[64,1,2176]{2,1,0:T(1,128)S(1)} %bitcast.11), channel_id=1, replica_groups={{0,2,4,6,8,10,12,14,16,18,20,22,24,26,28,30,32,34,36,38,40,42,44,46,48,..., dimensions={0} | all-to-all | bytes 1114112 | tf_op jit(solution)/shard_map/all_to_all | solution.py:617
  52.9 2.3 %collective-permute-start.4 = (f32[1088,128]{1,0:T(8,128)S(1)}, f32[1088,128]{1,0:T(8,128)S(1)}, u32[]{:S(2)}, u32[]{:S(2)}) collective-permute-start(f32[1088,128]{1,0:T(8,128)S(1)} %bitcast.9), channel_id=1, source_target_pairs={{0,1},{1,0},{2,3},{3,2},{4,5},{5,4},{6,7},{7,6},{8,9},{9,8},{10,11... | collective-permute-start | bytes 1671176 | tf_op jit(solution)/shard_map/ppermute | solution.py:619
  55.2 1.6 %collective-permute-done.4.far_ref = f32[1088,128]{1,0:T(8,128)S(1)} collective-permute-done((f32[1088,128]{1,0:T(8,128)S(1)}, f32[1088,128]{1,0:T(8,128)S(1)}, u32[]{:S(2)}, u32[]{:S(2)}) %collective-permute-start.4) | collective-permute-done | bytes 557088 | tf_op jit(solution)/shard_map/ppermute | solution.py:619
  56.8 4.5 %gradient.1 = (f32[1,64]{1,0:T(1,128)}, f32[1]{0:T(128)}) custom-call(f32[1088,128]{1,0:T(8,128)S(1)} %bitcast.10, f32[1088,128]{1,0:T(8,128)S(1)} %collective-permute-done.4.far_ref, f32[128,128]{1,0:T(8,128)S(1)} %coupling.1.coupling_ref, f32[1,32]{1,0:T(1,128)} %bitcast.13, f32[8,128]{1,0:T(8,128)S(1)} %get-tuple-element.13.extra_ref), custom_call_target="tpu_custom_call" | custom-call | tf_op jit(solution)/shard_map/gradient/pallas_call | solution.py:587
  (1 shorter events, 0.0 us)
Async XLA Ops:
  8.9 3.6 %collective-permute-start = (f32[4,264,128]{2,1,0:T(8,128)S(1)}, f32[4,264,128]{2,1,0:T(8,128)S(1)}, u32[]{:S(2)}, u32[]{:S(2)}) collective-permute-start(f32[4,264,128]{2,1,0:T(8,128)S(1)} %get-tuple-element.11), channel_id=1, source_target_pairs={{0,1},{1,0},{2,3},{3,2},{4,5},{5,4},{6,7},{7,6},{8,9},{9,8},{10,11... | collective-permute-start | bytes 1622024 | tf_op jit(solution)/shard_map/ppermute | solution.py:608
  12.5 8.9 %collective-permute-start.3 = (f32[264,128]{1,0:T(8,128)S(1)}, f32[264,128]{1,0:T(8,128)S(1)}, u32[]{:S(2)}, u32[]{:S(2)}) collective-permute-start(f32[264,128]{1,0:T(8,128)S(1)} %get-tuple-element.17), channel_id=1, source_target_pairs={{0,6},{1,7},{2,0},{3,1},{4,2},{5,3},{6,4},{7,5},{8,14},{9,15},{10,... | collective-permute-start | bytes 405512 | tf_op jit(solution)/shard_map/ppermute | solution.py:612
  15.4 6.1 %collective-permute-start.2 = (f32[264,128]{1,0:T(8,128)S(1)}, f32[264,128]{1,0:T(8,128)S(1)}, u32[]{:S(2)}, u32[]{:S(2)}) collective-permute-start(f32[264,128]{1,0:T(8,128)S(1)} %get-tuple-element.18), channel_id=1, source_target_pairs={{0,4},{1,5},{2,6},{3,7},{4,0},{5,1},{6,2},{7,3},{8,12},{9,13},{10,... | collective-permute-start | bytes 405512 | tf_op jit(solution)/shard_map/ppermute | solution.py:612
  15.4 9.3 %collective-permute-start.1 = (f32[264,128]{1,0:T(8,128)S(1)}, f32[264,128]{1,0:T(8,128)S(1)}, u32[]{:S(2)}, u32[]{:S(2)}) collective-permute-start(f32[264,128]{1,0:T(8,128)S(1)} %get-tuple-element.19), channel_id=1, source_target_pairs={{0,2},{1,3},{2,4},{3,5},{4,6},{5,7},{6,0},{7,1},{8,10},{9,11},{10,... | collective-permute-start | bytes 405512 | tf_op jit(solution)/shard_map/ppermute | solution.py:612
  52.9 3.8 %collective-permute-start.4 = (f32[1088,128]{1,0:T(8,128)S(1)}, f32[1088,128]{1,0:T(8,128)S(1)}, u32[]{:S(2)}, u32[]{:S(2)}) collective-permute-start(f32[1088,128]{1,0:T(8,128)S(1)} %bitcast.9), channel_id=1, source_target_pairs={{0,1},{1,0},{2,3},{3,2},{4,5},{5,4},{6,7},{7,6},{8,9},{9,8},{10,11... | collective-permute-start | bytes 1671176 | tf_op jit(solution)/shard_map/ppermute | solution.py:619
